TPU v7x, 32 devices: a whole 2x2x4 slice. The times are simulated.
32 devices in a mesh: dp: 4 (over x, core), expert: 8 (over z, y).
Axes of the slice: x: 2, y: 2, z: 4, core: 2. Of those that a mesh axis runs over, the one named last changes fastest.
Arguments:
- tokens: bfloat16 [512, 2048], P(('dp', 'expert')), may hold values from -6 to 6
- out_grad: bfloat16 [512, 2048], P(('dp', 'expert')), may hold values from -6 to 6
- expert_ids: int32 [512, 8], P(('dp', 'expert')), may hold values from 0 to 63, all different within a row; in each aligned block of 16 rows (0 to 15, 16 to 31, ...) at most 4 rows name the same one
- probs: bfloat16 [512, 8], P(('dp', 'expert')), may hold values from 0.049804688 to 0.5
- w_gate: bfloat16 [64, 2048, 384], P('expert'), may hold values from -0.125 to 0.125
- w_up: bfloat16 [64, 2048, 384], P('expert'), may hold values from -0.125 to 0.125
- w_down: bfloat16 [64, 2048, 384], P('expert'), may hold values from -0.3125 to 0.3125
Outputs:
- token_grad: bfloat16 [512, 2048], P(('dp', 'expert'))
- prob_grad: bfloat16 [512, 8], P(('dp', 'expert'))
- gate_grad: float32 [64, 2048, 384], P('expert', 'dp')
- up_grad: float32 [64, 2048, 384], P('expert', 'dp')
- down_grad: float32 [64, 2048, 384], P('expert', 'dp')
Inputs may be any that keep to these rules, and one draw needn't show every extreme that they name: `expert_ids`: each row names 8 different experts. Within each aligned block of 16 rows (the rows of one device) no expert is named by more than 4 rows, and that bound is reached in some blocks.
All inputs are finite; a program needn't handle non-finite values.
Results may differ from a plain program's by a relative error of at most 0.017.
Values may be sent and summed in bfloat16 or wider, within the bound.
No kernel may reach another device: no remote copies, remote signals or barrier semaphores. Data moves between devices by JAX's collectives and lax.ppermute only.
A program may use at most 128 MiB of HBM per device.

v0:
```python
import functools

import jax
import jax.numpy as jnp
from jax import lax
from jax.experimental import pallas as pl
from jax.experimental.pallas import tpu as pltpu
from jax.sharding import PartitionSpec as P


F32 = jnp.float32
BF16 = jnp.bfloat16
LANES = 128
HELD = ((2, 3, 6, 7), (4, 5, 1, 0))
BLOCKS = 8
KERNEL_VMEM = 30 * 1024 * 1024
WIDE_VMEM = 48 * 1024 * 1024
FETCH_VMEM = 12 * 1024 * 1024


def _contract(left, right, left_dim, right_dim):
    return lax.dot_general(
        left, right, (((left_dim,), (right_dim,)), ((), ())), preferred_element_type=F32
    )


def _order(size):
    earlier = lax.broadcasted_iota(jnp.int32, (size, size), 0)
    later = lax.broadcasted_iota(jnp.int32, (size, size), 1)
    return (earlier < later).astype(F32).astype(BF16)


def _select(meta_t, order, base, number, rows, top, start=0):
    named, weights = [], []
    for j in range(number):
        hit = meta_t[:top, :] == (base + lax.rem(start + j, number)).astype(F32)
        named.append(jnp.sum(jnp.where(hit, 1.0, 0.0), axis=0, keepdims=True))
        weights.append(
            jnp.sum(jnp.where(hit, meta_t[top : 2 * top, :], 0.0), axis=0, keepdims=True)
        )
    spread = jnp.concatenate(named + [named[0]] * (-number % 16), axis=0).astype(BF16)
    before = _contract(spread, order, 1, 0)
    row = lax.broadcasted_iota(jnp.int32, (rows, meta_t.shape[1]), 0).astype(F32)
    picks = []
    for j in range(number):
        slot = jnp.where(named[j] > 0.0, before[j : j + 1, :], -1.0)
        picks.append(jnp.where(row == slot, 1.0, 0.0))
    return picks, weights


def _pack_kernel(tokens, out_grad, ids_t, probs_t, packet):
    rows, width = tokens.shape
    packet[:, :width] = tokens[...]
    packet[:, width : 2 * width] = out_grad[...]
    top = ids_t.shape[0]
    meta = jnp.concatenate(
        [
            ids_t[...].astype(F32),
            probs_t[...].astype(F32),
            jnp.zeros((LANES - 2 * top, rows), F32),
        ],
        axis=0,
    )
    packet[:, 2 * width :] = meta.T.astype(BF16)


def _fetch_kernel(place, source, target, sem):
    own = target.shape[0]
    copies = [
        pltpu.make_async_copy(source.at[place[0] + j], target.at[j], sem.at[j]) for j in range(own)
    ]
    for copy in copies:
        copy.start()
    for copy in copies:
        copy.wait()


def _collect(core, sources, pieces, sems, block):
    copies = []
    for side, arrays in enumerate(sources):
        for i in range(BLOCKS // 2):
            array, index = arrays[i]
            at = lax.select(core == side, HELD[0][i], HELD[1][i]) * block
            rows = pl.ds(pl.multiple_of(at, block), block)
            for n, (columns, target) in enumerate(pieces):
                source = array.at[index, :, columns]
                copy = pltpu.make_async_copy(
                    source, target.at[rows, :], sems.at[n, side * (BLOCKS // 2) + i]
                )
                copy.start()
                copies.append(copy)
    return copies


def _hidden_kernel(place, *refs, own, rows, top, inputs, block):
    sources, (wg, wu, wd) = refs[:inputs], refs[inputs : inputs + 3]
    hidden, chosen, prob, packets, packet_sems, rows_x, rows_dy = refs[inputs + 3 :]
    _, width, ff = wg.shape
    if inputs == 1:
        arrivals = [pltpu.make_async_copy(sources[0], packets, packet_sems.at[0, 0])]
        arrivals[0].start()
    else:
        both = [[(array, i) for i in range(BLOCKS // 2)] for array in sources]
        whole = [(slice(None), packets)]
        arrivals = _collect(place[2], both, whole, packet_sems, block)
    for copy in arrivals:
        copy.wait()
    meta_t = packets[:, 2 * width :].astype(F32).T
    picks, weights = _select(meta_t, _order(packets.shape[0]), place[1], own, rows, top)
    for j in range(own):
        chosen[j * rows : (j + 1) * rows, :] = picks[j].astype(BF16)
    rows_x[...] = _contract(chosen[...], packets[:, :width], 1, 0).astype(BF16)
    rows_dy[...] = _contract(chosen[...], packets[:, width : 2 * width], 1, 0).astype(BF16)
    for j in range(own):
        at = slice(j * rows, (j + 1) * rows)
        scale = jnp.sum(picks[j] * weights[j], axis=1, keepdims=True)
        gate = _contract(rows_x[at, :], wg[j], 1, 0)
        up = _contract(rows_x[at, :], wu[j], 1, 0)
        back = _contract(rows_dy[at, :], wd[j], 1, 0)
        sigma = jax.nn.sigmoid(gate)
        silu = gate * sigma
        act = silu * up
        scaled_back = scale * back
        turned = scaled_back * up * sigma * (1.0 + gate * (1.0 - sigma))
        hidden[at, :ff] = turned.astype(BF16)
        hidden[at, ff : 2 * ff] = (scaled_back * silu).astype(BF16)
        hidden[at, 2 * ff :] = (scale * act).astype(BF16)
        score = jnp.sum(act * back, axis=1, keepdims=True)
        spread = jnp.sum(picks[j] * score, axis=0, keepdims=True)
        prob[j] = jnp.broadcast_to(spread, prob.shape[1:])


def _return_kernel(place, hidden, chosen, prob, wg, wu, keep, send, rows_out, *, own, rows, block):
    _, width, ff = wg.shape
    for j in range(own):
        at = slice(j * rows, (j + 1) * rows)
        back = _contract(hidden[at, :ff], wg[j], 1, 1)
        back = back + _contract(hidden[at, ff : 2 * ff], wu[j], 1, 1)
        rows_out[at, :] = back.astype(BF16)
    part = _contract(chosen[...], rows_out[...], 0, 0).astype(BF16)
    tokens = part.shape[0]
    lane = lax.broadcasted_iota(jnp.int32, (tokens, keep.shape[2] - width), 1)
    total = jnp.zeros(lane.shape, F32)
    for j in range(own):
        total = total + jnp.where(lane == place[1] + j, prob[j].T[:, :1], 0.0)
    total = total.astype(BF16)
    if send is None:
        for s in range(tokens // block):
            at = slice(s * block, (s + 1) * block)
            keep[s, :, :width] = part[at]
            keep[s, :, width:] = total[at]
        return
    first = place[0] == 0
    for s in range(tokens // block):
        low = slice(s * block, s * block + block // 2)
        high = slice(s * block + block // 2, (s + 1) * block)
        for value, lanes in ((part, slice(0, width)), (total, slice(width, None))):
            keep[s, :, lanes] = jnp.where(first, value[low], value[high])
            send[s, :, lanes] = jnp.where(first, value[high], value[low])


def _weights_kernel(place, *refs, local, rows, top, sets, halves, block, half, ff, inputs):
    sources, hidden = refs[:inputs], refs[inputs : inputs + sets * halves]
    rest = refs[inputs + sets * halves :]
    outs, (metas, xs, dys, sems, held, gate, up, down, in_sems, out_sems) = rest[:3], rest[3:]
    count, cols = xs.shape[1:]
    per_half = local // halves
    copies = []
    if inputs == sets:
        for s in range(sets):
            for n, (columns, target) in enumerate(
                (
                    (slice(0, cols), xs),
                    (slice(cols, 2 * cols), dys),
                    (slice(2 * cols, None), metas),
                )
            ):
                copy = pltpu.make_async_copy(
                    sources[s].at[:, columns], target.at[s], sems.at[s, n, 0]
                )
                copy.start()
                copies.append(copy)
    else:
        near, far = sources[:2], sources[2:]
        number = BLOCKS // 2
        both = [
            [[(array, i) for i in range(number)] for array in near],
            [[(far[2 * side + i % 2], i // 2) for i in range(number)] for side in range(2)],
        ]
        for s, (width, index) in enumerate(((2 * half, place[2]), (half, place[3]))):
            at = pl.multiple_of(index * cols, cols)
            pieces = (
                (pl.ds(at, cols), xs.at[s]),
                (pl.ds(pl.multiple_of(width + at, cols), cols), dys.at[s]),
                (slice(2 * width, None), metas.at[s]),
            )
            copies += _collect(place[3], both[s], pieces, sems.at[s], block)
    for at_half in range(halves):
        for s in range(sets):
            target = held.at[pl.ds(at_half * per_half, per_half), pl.ds(s * rows, rows), :]
            source = hidden[s * halves + at_half]
            copy = pltpu.make_async_copy(source, target, in_sems.at[at_half, s])
            copy.start()
            copies.append(copy)
    order = _order(count)
    for copy in copies:
        copy.wait()
    picks = []
    for s in range(sets):
        turned = metas[s].astype(F32).T
        picks.append(_select(turned, order, place[1], local, rows, top, place[0])[0])
    departures = []
    for j in range(local):
        index = lax.rem(place[0] + j, local)
        turned = []
        for source in (xs, dys):
            taken = [
                _contract(picks[s][j].astype(BF16), source[s], 1, 0).astype(BF16)
                for s in range(sets)
            ]
            turned.append(jnp.concatenate(taken, axis=0))
        for i, (buffer, left) in enumerate(
            ((gate, turned[0]), (up, turned[0]), (down, turned[1]))
        ):
            buffer[j] = _contract(left, held[j, :, i * ff : (i + 1) * ff], 0, 0)
            copy = pltpu.make_async_copy(buffer.at[j], outs[i].at[index], out_sems.at[i, j])
            copy.start()
            departures.append(copy)
    for copy in departures:
        copy.wait()


def _finish_kernel(ids_t, kept, *refs):
    *others, token_grad, prob_grad_t = refs
    total = kept[...].astype(F32)
    for other in others:
        total = total + other[...].astype(F32)
    width = token_grad.shape[1]
    token_grad[...] = total[:, :width].astype(BF16)
    score = total[:, width:].T
    expert = lax.broadcasted_iota(jnp.int32, score.shape, 0)
    found = [
        jnp.sum(jnp.where(expert == ids_t[k : k + 1, :], score, 0.0), axis=0, keepdims=True)
        for k in range(ids_t.shape[0])
    ]
    prob_grad_t[...] = jnp.concatenate(found, axis=0).astype(BF16)


def _cost(flops, nbytes):
    return pl.CostEstimate(flops=int(flops), bytes_accessed=int(nbytes), transcendentals=0)


def layer(tokens, out_grad, expert_ids, probs, w_gate, w_up, w_down):
    tok_rows, width = tokens.shape
    top = expert_ids.shape[1]
    local, _, ff = w_gate.shape
    ranks, groups = lax.axis_size("expert"), lax.axis_size("dp")
    experts = local * ranks
    slots = 2 * tok_rows * top // experts
    cols = width // groups
    paired = groups == 4 and ranks == 8 and local % 2 == 0
    pair = 2 if paired else 1
    sets = groups // pair
    own = local // pair
    count = pair * ranks * tok_rows
    rows = pair * ranks * slots
    dp, rank = lax.axis_index("dp"), lax.axis_index("expert")
    core = lax.rem(dp, pair)
    extra = -(-experts // LANES) * LANES
    devices = [(d, e) for d in range(groups) for e in range(ranks)]

    def move(value, target):
        pairs = []
        for d, e in devices:
            to = target(d, e)
            if to is not None:
                pairs.append((d * ranks + e, to[0] * ranks + to[1]))
        return lax.ppermute(value, ("dp", "expert"), pairs)

    def to_core(value):
        return move(value, lambda d, e: (d ^ 1, e))

    def to_chip(value):
        return move(value, lambda d, e: (d ^ 2, e))

    def to_rank(value, first, second):
        def target(d, e):
            off = second if d % 2 else first
            return None if off is None else (d, e ^ off)

        return move(value, target)

    first = core == 0

    vmem = pl.BlockSpec(memory_space=pltpu.VMEM)
    smem = pl.BlockSpec(memory_space=pltpu.SMEM)
    hbm = pl.BlockSpec(memory_space=pltpu.HBM)
    limit = pltpu.CompilerParams(vmem_limit_bytes=KERNEL_VMEM)
    packet = pl.pallas_call(
        _pack_kernel,
        out_shape=jax.ShapeDtypeStruct((tok_rows, 2 * width + LANES), BF16),
        in_specs=[vmem] * 4,
        out_specs=vmem,
        name="pack",
    )(tokens, out_grad, expert_ids.T, probs.T)
    half = width // sets
    if paired:
        other = to_core(packet)
        chip = jnp.where(
            first,
            jnp.concatenate([packet, other], axis=0),
            jnp.concatenate([other, packet], axis=0),
        )
        at = (1 - dp // pair) * half

        def slim(block):
            return jnp.concatenate(
                [
                    lax.dynamic_slice(block, (0, at), (block.shape[0], half)),
                    lax.dynamic_slice(block, (0, width + at), (block.shape[0], half)),
                    block[:, 2 * width :],
                ],
                axis=1,
            )

        near = to_rank(chip, 2, 4)
        side = to_rank(chip, 6, 1)
        near_side = to_rank(near, 1, 1)
        side_side = to_rank(side, 1, None)
        last_block = jnp.where(first, side_side, chip)
        far_a = to_chip(jnp.stack([slim(near), slim(side)]))
        far_b = to_chip(jnp.stack([slim(near_side), slim(last_block)]))
        held = jnp.stack([near, near_side, side, last_block])
        gathered = [held, to_core(held)]
    else:
        gathered = [lax.all_gather(packet, "expert", axis=0, tiled=True)]

    place = jnp.stack([core * own, rank * local + core * own, core]).astype(jnp.int32)
    mine = []
    for weight in (w_gate, w_up, w_down):
        mine.append(
            pl.pallas_call(
                _fetch_kernel,
                out_shape=jax.ShapeDtypeStruct((own, width, ff), BF16),
                in_specs=[smem, hbm],
                out_specs=vmem,
                scratch_shapes=[pltpu.SemaphoreType.DMA((own,))],
                compiler_params=pltpu.CompilerParams(vmem_limit_bytes=FETCH_VMEM),
                cost_estimate=_cost(width * ff * own, 4 * own * width * ff),
            )(place, weight)
        )
    block = pair * tok_rows
    hidden, chosen, prob = pl.pallas_call(
        functools.partial(
            _hidden_kernel, own=own, rows=rows, top=top, inputs=len(gathered), block=block
        ),
        out_shape=(
            jax.ShapeDtypeStruct((own * rows, 3 * ff), BF16),
            jax.ShapeDtypeStruct((own * rows, count), BF16),
            jax.ShapeDtypeStruct((own, 8, count), F32),
        ),
        in_specs=[smem] + [hbm] * len(gathered) + [vmem] * 3,
        out_specs=(vmem, vmem, vmem),
        scratch_shapes=[
            pltpu.VMEM((count, 2 * width + LANES), BF16),
            pltpu.SemaphoreType.DMA((1, BLOCKS)),
        ]
        + [pltpu.VMEM((own * rows, width), BF16)] * 2,
        compiler_params=limit,
        cost_estimate=_cost(6 * own * rows * width * ff, 6 * own * width * ff),
        name="hidden",
    )(place, *gathered, *mine)

    if paired:
        sources = gathered + [far_a, far_b, to_core(far_a), to_core(far_b)]
        hidden_far = to_chip(hidden)
        hidden_all = [hidden, to_core(hidden), hidden_far, to_core(hidden_far)]
    else:
        by_owner = gathered[0][:, : 2 * width].reshape(count, 2, groups, cols)
        by_owner = jnp.moveaxis(by_owner, 2, 0).reshape(groups, count, 2 * cols)
        moved = lax.all_to_all(by_owner, "dp", 0, 0, tiled=True)
        metas = lax.all_gather(gathered[0][:, 2 * width :], "dp", axis=0)
        sources = [jnp.concatenate([moved[s], metas[s]], axis=1) for s in range(sets)]
        spread = lax.all_gather(hidden, "dp", axis=0)
        hidden_all = [spread[s] for s in range(sets)]

    kernel = functools.partial(_return_kernel, own=own, rows=rows, block=block)
    if pair == 1:
        kernel = functools.partial(
            lambda *refs, call: call(*refs[:7], None, *refs[7:]), call=kernel
        )
    piece = jax.ShapeDtypeStruct((ranks, tok_rows, width + extra), BF16)
    parts = pl.pallas_call(
        kernel,
        out_shape=(piece,) * pair,
        in_specs=[smem] + [vmem] * 5,
        out_specs=(vmem,) * pair,
        scratch_shapes=[pltpu.VMEM((own * rows, width), BF16)],
        compiler_params=limit,
        cost_estimate=_cost(8 * own * rows * width * ff, 4 * own * width * ff),
        name="contributions",
    )(place, hidden, chosen, prob, *mine[:2])

    if paired:
        theirs = to_core(parts[1])
        summed = (parts[0].astype(F32) + theirs.astype(F32)).astype(BF16)
        back = [summed[0]]
        back += [to_rank(summed[i], i, i) for i in range(ranks - 1, 0, -1)]
    else:
        back = lax.all_to_all(parts[0], "expert", 0, 0, tiled=True)
        back = [back[i] for i in range(ranks)]
    place_all = jnp.stack([core * own, rank * local, dp, core]).astype(jnp.int32)
    shape = jax.ShapeDtypeStruct((local, cols, ff), F32)
    hidden_all = [value.reshape(own, rows, 3 * ff) for value in hidden_all]
    gate_grad, up_grad, down_grad = pl.pallas_call(
        functools.partial(
            _weights_kernel,
            local=local,
            rows=rows,
            top=top,
            sets=sets,
            halves=pair,
            block=block,
            half=half,
            ff=ff,
            inputs=len(sources),
        ),
        out_shape=(shape, shape, shape),
        in_specs=[smem] + [hbm] * (len(sources) + len(hidden_all)),
        out_specs=(hbm, hbm, hbm),
        scratch_shapes=[
            pltpu.VMEM((sets, count, LANES), BF16),
            pltpu.VMEM((sets, count, cols), BF16),
            pltpu.VMEM((sets, count, cols), BF16),
            pltpu.SemaphoreType.DMA((sets, 3, BLOCKS)),
            pltpu.VMEM((local, sets * rows, 3 * ff), BF16),
        ]
        + [pltpu.VMEM((local, cols, ff), F32)] * 3
        + [pltpu.SemaphoreType.DMA((pair, sets)), pltpu.SemaphoreType.DMA((3, local))],
        compiler_params=pltpu.CompilerParams(vmem_limit_bytes=WIDE_VMEM),
        cost_estimate=_cost(6 * local * sets * rows * cols * ff, 12 * local * cols * ff),
        name="weight_grads",
    )(place_all, *sources, *hidden_all)
    token_grad, prob_grad_t = pl.pallas_call(
        _finish_kernel,
        out_shape=(
            jax.ShapeDtypeStruct((tok_rows, width), BF16),
            jax.ShapeDtypeStruct((top, tok_rows), BF16),
        ),
        in_specs=[vmem] * (1 + len(back)),
        out_specs=(vmem, vmem),
        name="finish",
    )(expert_ids.T, *back)
    prob_grad = prob_grad_t.T
    return (token_grad, prob_grad, gate_grad, up_grad, down_grad)


def solution(mesh):
    placed = (
        P(("dp", "expert"), None),
        P(("dp", "expert"), None),
        P(("dp", "expert"), None),
        P(("dp", "expert"), None),
        P("expert", None, None),
        P("expert", None, None),
        P("expert", None, None),
    )
    return jax.shard_map(
        layer,
        mesh=mesh,
        in_specs=placed,
        out_specs=(
            P(("dp", "expert"), None),
            P(("dp", "expert"), None),
            P("expert", "dp", None),
            P("expert", "dp", None),
            P("expert", "dp", None),
        ),
        check_vma=False,
    )
```

profile of v0, /device:TPU:0, one launch (start us, length us, event | category | flops | bytes accessed | tf_op | source)
XLA Modules:
  0.0 117.9 jit_solution(8396381686054137190)
XLA Ops:
  0.6 1.6 %pack.1 = bf16[16,4224]{1,0:T(8,128)(2,1)} custom-call(bf16[16,2048]{1,0:T(8,128)(2,1)} %tokens.1, bf16[16,2048]{1,0:T(8,128)(2,1)} %out_grad.1, s32[8,16]{1,0:T(8,128)} %bitcast.46, bf16[8,16]{1,0:T(8,128)(2,1)} %bitcast.48), custom_call_target="tpu_custom_call" | custom-call | tf_op jit(solution)/shard_map/pack/pallas_call | solution.py:299
  2.2 0.5 collective-permute-start
  2.7 1.2 %collective-permute-done = bf16[16,4224]{1,0:T(8,128)(2,1)S(1)} collective-permute-done((bf16[16,4224]{1,0:T(8,128)(2,1)}, bf16[16,4224]{1,0:T(8,128)(2,1)S(1)}, u32[]{:S(2)}, u32[]{:S(2)}) %collective-permute-start) | collective-permute-done | bytes 135200 | tf_op jit(solution)/shard_map/ppermute | solution.py:278
  3.9 1.0 maximum_select_fusion
  5.0 5.0 %collective-permute-start.3 = (bf16[32,4224]{1,0:T(8,128)(2,1)S(1)}, bf16[32,4224]{1,0:T(8,128)(2,1)S(1)}, u32[]{:S(2)}, u32[]{:S(2)}) collective-permute-start(bf16[32,4224]{1,0:T(8,128)(2,1)S(1)} %maximum_select_fusion), channel_id=1, source_target_pairs={{0,6},{1,7},{2,4},{3,5},{4,2},{5,3},{6,0},{7,1},{8,9},{9,8},{10,11... | collective-permute-start | bytes 811016 | tf_op jit(solution)/shard_map/ppermute | solution.py:278
  10.0 0.0 collective-permute-start.1
  10.0 0.1 pad_add_fusion.place
  10.1 4.6 %copy-done = bf16[8,2048,384]{2,1,0:T(8,128)(2,1)S(1)} copy-done((bf16[8,2048,384]{2,1,0:T(8,128)(2,1)S(1)}, bf16[8,2048,384]{2,1,0:T(8,128)(2,1)}, u32[]{:S(2)}) %copy-start) | copy-done | bytes 12582936
  14.6 1.0 shard_map.110.refs_2_.wg
  15.7 3.6 %copy-done.1 = bf16[8,2048,384]{2,1,0:T(8,128)(2,1)S(1)} copy-done((bf16[8,2048,384]{2,1,0:T(8,128)(2,1)S(1)}, bf16[8,2048,384]{2,1,0:T(8,128)(2,1)}, u32[]{:S(2)}) %copy-start.1) | copy-done | bytes 12582936
  19.2 1.0 shard_map.111.refs_3_.wu
  20.2 0.0 copy-start.2
  20.2 4.6 %copy-done.2 = bf16[8,2048,384]{2,1,0:T(8,128)(2,1)S(1)} copy-done((bf16[8,2048,384]{2,1,0:T(8,128)(2,1)S(1)}, bf16[8,2048,384]{2,1,0:T(8,128)(2,1)}, u32[]{:S(2)}) %copy-start.2) | copy-done | bytes 12582936
  24.8 1.0 shard_map.112.refs_4_
  25.8 0.0 collective-permute-done.3
  25.9 3.4 %collective-permute-start.4 = (bf16[32,4224]{1,0:T(8,128)(2,1)S(1)}, bf16[32,4224]{1,0:T(8,128)(2,1)S(1)}, u32[]{:S(2)}, u32[]{:S(2)}) collective-permute-start(bf16[32,4224]{1,0:T(8,128)(2,1)S(1)} %collective-permute-done.3), channel_id=1, source_target_pairs={{0,1},{1,0},{2,3},{3,2},{4,5},{5,4},{6,7},{7,6},{16,17},{17,16},{1... | collective-permute-start | bytes 811016 | tf_op jit(solution)/shard_map/ppermute | solution.py:278
  29.3 0.0 collective-permute-done.1
  29.4 0.6 collective-permute-start.2
  29.9 5.2 %collective-permute-done.4 = bf16[32,4224]{1,0:T(8,128)(2,1)S(1)} collective-permute-done((bf16[32,4224]{1,0:T(8,128)(2,1)S(1)}, bf16[32,4224]{1,0:T(8,128)(2,1)S(1)}, u32[]{:S(2)}, u32[]{:S(2)}) %collective-permute-start.4) | collective-permute-done | bytes 270368 | tf_op jit(solution)/shard_map/ppermute | solution.py:278
  35.2 0.0 copy-done.3
  35.2 0.1 broadcast_select_fusion
  35.2 2.8 %collective-permute-done.2 = bf16[32,4224]{1,0:T(8,128)(2,1)S(1)} collective-permute-done((bf16[32,4224]{1,0:T(8,128)(2,1)S(1)}, bf16[32,4224]{1,0:T(8,128)(2,1)S(1)}, u32[]{:S(2)}, u32[]{:S(2)}) %collective-permute-start.2) | collective-permute-done | bytes 270368 | tf_op jit(solution)/shard_map/ppermute | solution.py:278
  38.1 0.2 pad_maximum_fusion.refs_0_
  38.2 0.1 collective-permute-start.5
  38.4 1.6 %collective-permute-start.14 = (bf16[2,32,2176]{2,1,0:T(8,128)(2,1)S(1)}, bf16[2,32,2176]{2,1,0:T(8,128)(2,1)}, u32[]{:S(2)}, u32[]{:S(2)}) collective-permute-start(bf16[2,32,2176]{2,1,0:T(8,128)(2,1)S(1)} %pad_maximum_fusion.1), channel_id=1, source_target_pairs={{0,16},{1,17},{2,18},{3,19},{4,20},{5,21},{6,22},{7,23},{8,24},{9,... | collective-permute-start | bytes 835592 | tf_op jit(solution)/shard_map/ppermute | solution.py:278
  40.0 1.0 collective-permute-done.5.refs_1_
  41.0 4.8 %hidden.1 = (bf16[256,1152]{1,0:T(8,128)(2,1)S(1)}, bf16[256,256]{1,0:T(8,128)(2,1)S(1)}, f32[4,8,256]{2,1,0:T(8,128)S(1)}) custom-call(s32[3]{0:T(128)S(1)} %pad_add_fusion.place, bf16[4,32,4224]{2,1,0:T(8,128)(2,1)S(1)} %pad_maximum_fusion.refs_0_, bf16[4,32,4224]{2,1,0:T(8,128)(2,1)S(1)} %collective-permute-done.5.refs_1_, ...), custom_call_target="tpu_custom_call" | custom-call | flops 1207959552 | bytes 18874368 | tf_op jit(solution)/shard_map/hidden/pallas_call | solution.py:353
  45.8 5.0 %contributions.1 = (bf16[8,16,2176]{2,1,0:T(8,128)(2,1)S(1)}, bf16[8,16,2176]{2,1,0:T(8,128)(2,1)S(1)}) custom-call(s32[3]{0:T(128)S(1)} %pad_add_fusion.place, bf16[256,1152]{1,0:T(8,128)(2,1)S(1)} %get-tuple-element.15.hidden, bf16[256,256]{1,0:T(8,128)(2,1)S(1)} %get-tuple-element.16.chosen, f32[4,8,256]{2,1,0:T(8,128)S(1)} %get-tuple-element.17.prob, ...), custom_call_target="tpu_custom_call" | custom-call | flops 1610612736 | bytes 12582912 | tf_op jit(solution)/shard_map/contributions/pallas_call | solution.py:393
  50.7 0.2 collective-permute-start.6
  51.0 1.6 %collective-permute-start.15 = (bf16[2,32,2176]{2,1,0:T(8,128)(2,1)S(1)}, bf16[2,32,2176]{2,1,0:T(8,128)(2,1)}, u32[]{:S(2)}, u32[]{:S(2)}) collective-permute-start(bf16[2,32,2176]{2,1,0:T(8,128)(2,1)S(1)} %pad_maximum_fusion.2), channel_id=1, source_target_pairs={{0,16},{1,17},{2,18},{3,19},{4,20},{5,21},{6,22},{7,23},{8,24},{9,... | collective-permute-start | bytes 835592 | tf_op jit(solution)/shard_map/ppermute | solution.py:278
  52.5 0.5 collective-permute-start.19
  53.1 0.0 collective-permute-start.18
  53.1 0.0 collective-permute-done.6
  53.1 0.1 add_convert_fusion
  53.2 19.4 %collective-permute-done.19 = bf16[256,1152]{1,0:T(8,128)(2,1)S(1)} collective-permute-done((bf16[256,1152]{1,0:T(8,128)(2,1)S(1)}, bf16[256,1152]{1,0:T(8,128)(2,1)S(1)}, u32[]{:S(2)}, u32[]{:S(2)}) %collective-permute-start.19) | collective-permute-done | bytes 589856 | tf_op jit(solution)/shard_map/ppermute | solution.py:278
  72.6 0.0 collective-permute-start.20
  72.6 0.7 slice_bitcast_fusion
  73.3 0.6 collective-permute-start.13
  73.9 0.0 collective-permute-done.14.refs_2_
  73.9 2.0 %collective-permute-start.12 = (bf16[16,2176]{1,0:T(8,128)(2,1)S(1)}, bf16[16,2176]{1,0:T(8,128)(2,1)S(1)}, u32[]{:S(2)}, u32[]{:S(2)}) collective-permute-start(bf16[16,2176]{1,0:T(8,128)(2,1)S(1)} %get-tuple-element.26), channel_id=1, source_target_pairs={{0,2},{1,3},{2,0},{3,1},{4,6},{5,7},{6,4},{7,5},{8,10},{9,11},{10,... | collective-permute-start | bytes 208904 | tf_op jit(solution)/shard_map/ppermute | solution.py:278
  75.9 0.0 collective-permute-done.15.refs_3_
  75.9 0.9 collective-permute-start.11
  76.8 1.1 collective-permute-done.13.refs_6_
  77.9 0.3 collective-permute-start.10
  78.2 0.2 collective-permute-done.12.refs_5_
  78.5 0.0 collective-permute-start.16
  78.5 2.6 %collective-permute-done.11.refs_4_ = bf16[16,2176]{1,0:T(8,128)(2,1)S(1)} collective-permute-done((bf16[16,2176]{1,0:T(8,128)(2,1)S(1)}, bf16[16,2176]{1,0:T(8,128)(2,1)S(1)}, u32[]{:S(2)}, u32[]{:S(2)}) %collective-permute-start.11) | collective-permute-done | bytes 69664 | tf_op jit(solution)/shard_map/ppermute | solution.py:278
  81.1 0.0 collective-permute-start.17
  81.1 3.2 %collective-permute-done.10.refs_3_ = bf16[16,2176]{1,0:T(8,128)(2,1)S(1)} collective-permute-done((bf16[16,2176]{1,0:T(8,128)(2,1)S(1)}, bf16[16,2176]{1,0:T(8,128)(2,1)S(1)}, u32[]{:S(2)}, u32[]{:S(2)}) %collective-permute-start.10) | collective-permute-done | bytes 69664 | tf_op jit(solution)/shard_map/ppermute | solution.py:278
  84.3 0.4 collective-permute-start.9
  84.6 6.6 %collective-permute-done.9.refs_2_ = bf16[16,2176]{1,0:T(8,128)(2,1)S(1)} collective-permute-done((bf16[16,2176]{1,0:T(8,128)(2,1)S(1)}, bf16[16,2176]{1,0:T(8,128)(2,1)S(1)}, u32[]{:S(2)}, u32[]{:S(2)}) %collective-permute-start.9) | collective-permute-done | bytes 69664 | tf_op jit(solution)/shard_map/ppermute | solution.py:278
  91.3 0.7 collective-permute-start.8
  92.0 6.0 %collective-permute-done.8.refs_1_ = bf16[16,2176]{1,0:T(8,128)(2,1)S(1)} collective-permute-done((bf16[16,2176]{1,0:T(8,128)(2,1)S(1)}, bf16[16,2176]{1,0:T(8,128)(2,1)S(1)}, u32[]{:S(2)}, u32[]{:S(2)}) %collective-permute-start.8) | collective-permute-done | bytes 69664 | tf_op jit(solution)/shard_map/ppermute | solution.py:278
  98.0 0.5 collective-permute-start.7
  98.5 0.1 pad_add_fusion.1.place
  98.6 6.4 %collective-permute-done.7.refs_0_ = bf16[16,2176]{1,0:T(8,128)(2,1)S(1)} collective-permute-done((bf16[16,2176]{1,0:T(8,128)(2,1)S(1)}, bf16[16,2176]{1,0:T(8,128)(2,1)S(1)}, u32[]{:S(2)}, u32[]{:S(2)}) %collective-permute-start.7) | collective-permute-done | bytes 69664 | tf_op jit(solution)/shard_map/ppermute | solution.py:278
  105.0 0.0 copy-start.10
  105.0 0.6 copy-done.10
  105.6 2.0 %finish.1 = (bf16[16,2048]{1,0:T(8,128)(2,1)}, bf16[8,16]{1,0:T(8,128)(2,1)}) custom-call(s32[8,16]{1,0:T(8,128)} %bitcast.47, bf16[16,2176]{1,0:T(8,128)(2,1)} %get-tuple-element.32.kept, bf16[16,2176]{1,0:T(8,128)(2,1)} %copy-done.10, bf16[16,2176]{1,0:T(8,128)(2,1)} %copy-done.9, bf16[16,2176]{1,0:T(8,128)(2,1)} %copy-done.8, bf16[16,2176]{1,0:T(8,128)(2,1)} %copy-done.7, ...), custom_call_target="tpu_custom_call" | custom-call | tf_op jit(solution)/shard_map/finish/pallas_call | solution.py:444
  107.6 0.0 collective-permute-done.16.refs_4_
  107.6 0.0 collective-permute-done.17.refs_5_
  107.6 0.0 collective-permute-done.18
  107.7 0.0 collective-permute-done.20
  107.7 10.2 %weight_grads.1 = (f32[8,512,384]{2,1,0:T(8,128)}, f32[8,512,384]{2,1,0:T(8,128)}, f32[8,512,384]{2,1,0:T(8,128)}) custom-call(s32[4]{0:T(128)S(1)} %pad_add_fusion.1.place, bf16[4,32,4224]{2,1,0:T(8,128)(2,1)S(1)} %pad_maximum_fusion.refs_0_, bf16[4,32,4224]{2,1,0:T(8,128)(2,1)S(1)} %collective-permute-done.5.refs_1_, ...), custom_call_target="tpu_custom_call" | custom-call | flops 1207959552 | bytes 18874368 | tf_op jit(solution)/shard_map/weight_grads/pallas_call | solution.py:415
  (29 shorter events, 0.2 us)
Async XLA Ops:
  2.2 1.7 %collective-permute-start = (bf16[16,4224]{1,0:T(8,128)(2,1)}, bf16[16,4224]{1,0:T(8,128)(2,1)S(1)}, u32[]{:S(2)}, u32[]{:S(2)}) collective-permute-start(bf16[16,4224]{1,0:T(8,128)(2,1)} %pack.1), channel_id=1, source_target_pairs={{0,8},{1,9},{2,10},{3,11},{4,12},{5,13},{6,14},{7,15},{8,0},{9,1},... | collective-permute-start | bytes 405512 | tf_op jit(solution)/shard_map/ppermute | solution.py:278
  5.0 20.9 %collective-permute-start.3 = (bf16[32,4224]{1,0:T(8,128)(2,1)S(1)}, bf16[32,4224]{1,0:T(8,128)(2,1)S(1)}, u32[]{:S(2)}, u32[]{:S(2)}) collective-permute-start(bf16[32,4224]{1,0:T(8,128)(2,1)S(1)} %maximum_select_fusion), channel_id=1, source_target_pairs={{0,6},{1,7},{2,4},{3,5},{4,2},{5,3},{6,0},{7,1},{8,9},{9,8},{10,11... | collective-permute-start | bytes 811016 | tf_op jit(solution)/shard_map/ppermute | solution.py:278
  10.0 19.3 %collective-permute-start.1 = (bf16[32,4224]{1,0:T(8,128)(2,1)S(1)}, bf16[32,4224]{1,0:T(8,128)(2,1)S(1)}, u32[]{:S(2)}, u32[]{:S(2)}) collective-permute-start(bf16[32,4224]{1,0:T(8,128)(2,1)S(1)} %maximum_select_fusion), channel_id=1, source_target_pairs={{0,2},{1,3},{2,0},{3,1},{4,6},{5,7},{6,4},{7,5},{8,12},{9,13},{10,... | collective-permute-start | bytes 811016 | tf_op jit(solution)/shard_map/ppermute | solution.py:278
  10.1 4.6 %copy-start = (bf16[8,2048,384]{2,1,0:T(8,128)(2,1)S(1)}, bf16[8,2048,384]{2,1,0:T(8,128)(2,1)}, u32[]{:S(2)}) copy-start(bf16[8,2048,384]{2,1,0:T(8,128)(2,1)} %source.3) | copy-start | bytes 37748740
  14.6 4.6 %copy-start.1 = (bf16[8,2048,384]{2,1,0:T(8,128)(2,1)S(1)}, bf16[8,2048,384]{2,1,0:T(8,128)(2,1)}, u32[]{:S(2)}) copy-start(bf16[8,2048,384]{2,1,0:T(8,128)(2,1)} %source.4) | copy-start | bytes 37748740
  20.2 4.6 %copy-start.2 = (bf16[8,2048,384]{2,1,0:T(8,128)(2,1)S(1)}, bf16[8,2048,384]{2,1,0:T(8,128)(2,1)}, u32[]{:S(2)}) copy-start(bf16[8,2048,384]{2,1,0:T(8,128)(2,1)} %source.5) | copy-start | bytes 37748740
  24.8 10.3 %copy-start.3 = (bf16[16,4224]{1,0:T(8,128)(2,1)S(1)}, bf16[16,4224]{1,0:T(8,128)(2,1)}, u32[]{:S(2)}) copy-start(bf16[16,4224]{1,0:T(8,128)(2,1)} %pack.1) | copy-start | bytes 405508
  25.9 9.3 %collective-permute-start.4 = (bf16[32,4224]{1,0:T(8,128)(2,1)S(1)}, bf16[32,4224]{1,0:T(8,128)(2,1)S(1)}, u32[]{:S(2)}, u32[]{:S(2)}) collective-permute-start(bf16[32,4224]{1,0:T(8,128)(2,1)S(1)} %collective-permute-done.3), channel_id=1, source_target_pairs={{0,1},{1,0},{2,3},{3,2},{4,5},{5,4},{6,7},{7,6},{16,17},{17,16},{1... | collective-permute-start | bytes 811016 | tf_op jit(solution)/shard_map/ppermute | solution.py:278
  29.4 8.7 %collective-permute-start.2 = (bf16[32,4224]{1,0:T(8,128)(2,1)S(1)}, bf16[32,4224]{1,0:T(8,128)(2,1)S(1)}, u32[]{:S(2)}, u32[]{:S(2)}) collective-permute-start(bf16[32,4224]{1,0:T(8,128)(2,1)S(1)} %collective-permute-done.1), channel_id=1, source_target_pairs={{0,1},{1,0},{2,3},{3,2},{4,5},{5,4},{6,7},{7,6},{8,9},{9,8},{10,11... | collective-permute-start | bytes 811016 | tf_op jit(solution)/shard_map/ppermute | solution.py:278
  38.2 2.8 %collective-permute-start.5 = (bf16[4,32,4224]{2,1,0:T(8,128)(2,1)S(1)}, bf16[4,32,4224]{2,1,0:T(8,128)(2,1)S(1)}, u32[]{:S(2)}, u32[]{:S(2)}) collective-permute-start(bf16[4,32,4224]{2,1,0:T(8,128)(2,1)S(1)} %pad_maximum_fusion.refs_0_), channel_id=1, source_target_pairs={{0,8},{1,9},{2,10},{3,11},{4,12},{5,13},{6,14},{7,15},{8,0},{9,1},... | collective-permute-start | bytes 3244040 | tf_op jit(solution)/shard_map/ppermute | solution.py:278
  38.4 35.5 %collective-permute-start.14 = (bf16[2,32,2176]{2,1,0:T(8,128)(2,1)S(1)}, bf16[2,32,2176]{2,1,0:T(8,128)(2,1)}, u32[]{:S(2)}, u32[]{:S(2)}) collective-permute-start(bf16[2,32,2176]{2,1,0:T(8,128)(2,1)S(1)} %pad_maximum_fusion.1), channel_id=1, source_target_pairs={{0,16},{1,17},{2,18},{3,19},{4,20},{5,21},{6,22},{7,23},{8,24},{9,... | collective-permute-start | bytes 835592 | tf_op jit(solution)/shard_map/ppermute | solution.py:278
  50.7 2.4 %collective-permute-start.6 = (bf16[8,16,2176]{2,1,0:T(8,128)(2,1)S(1)}, bf16[8,16,2176]{2,1,0:T(8,128)(2,1)S(1)}, u32[]{:S(2)}, u32[]{:S(2)}) collective-permute-start(bf16[8,16,2176]{2,1,0:T(8,128)(2,1)S(1)} %get-tuple-element.19), channel_id=1, source_target_pairs={{0,8},{1,9},{2,10},{3,11},{4,12},{5,13},{6,14},{7,15},{8,0},{9,1},... | collective-permute-start | bytes 1671176 | tf_op jit(solution)/shard_map/ppermute | solution.py:278
  51.0 24.9 %collective-permute-start.15 = (bf16[2,32,2176]{2,1,0:T(8,128)(2,1)S(1)}, bf16[2,32,2176]{2,1,0:T(8,128)(2,1)}, u32[]{:S(2)}, u32[]{:S(2)}) collective-permute-start(bf16[2,32,2176]{2,1,0:T(8,128)(2,1)S(1)} %pad_maximum_fusion.2), channel_id=1, source_target_pairs={{0,16},{1,17},{2,18},{3,19},{4,20},{5,21},{6,22},{7,23},{8,24},{9,... | collective-permute-start | bytes 835592 | tf_op jit(solution)/shard_map/ppermute | solution.py:278
  52.5 20.1 %collective-permute-start.19 = (bf16[256,1152]{1,0:T(8,128)(2,1)S(1)}, bf16[256,1152]{1,0:T(8,128)(2,1)S(1)}, u32[]{:S(2)}, u32[]{:S(2)}) collective-permute-start(bf16[256,1152]{1,0:T(8,128)(2,1)S(1)} %get-tuple-element.15.hidden), channel_id=1, source_target_pairs={{0,16},{1,17},{2,18},{3,19},{4,20},{5,21},{6,22},{7,23},{8,24},{9,... | collective-permute-start | bytes 1769480 | tf_op jit(solution)/shard_map/ppermute | solution.py:278
  53.1 54.6 %collective-permute-start.18 = (bf16[256,1152]{1,0:T(8,128)(2,1)S(1)}, bf16[256,1152]{1,0:T(8,128)(2,1)}, u32[]{:S(2)}, u32[]{:S(2)}) collective-permute-start(bf16[256,1152]{1,0:T(8,128)(2,1)S(1)} %get-tuple-element.15.hidden), channel_id=1, source_target_pairs={{0,8},{1,9},{2,10},{3,11},{4,12},{5,13},{6,14},{7,15},{8,0},{9,1},... | collective-permute-start | bytes 1769480 | tf_op jit(solution)/shard_map/ppermute | solution.py:278
  72.6 35.0 %collective-permute-start.20 = (bf16[256,1152]{1,0:T(8,128)(2,1)S(1)}, bf16[256,1152]{1,0:T(8,128)(2,1)}, u32[]{:S(2)}, u32[]{:S(2)}) collective-permute-start(bf16[256,1152]{1,0:T(8,128)(2,1)S(1)} %collective-permute-done.19), channel_id=1, source_target_pairs={{0,8},{1,9},{2,10},{3,11},{4,12},{5,13},{6,14},{7,15},{8,0},{9,1},... | collective-permute-start | bytes 1769480 | tf_op jit(solution)/shard_map/ppermute | solution.py:278
  73.3 4.6 %collective-permute-start.13 = (bf16[16,2176]{1,0:T(8,128)(2,1)S(1)}, bf16[16,2176]{1,0:T(8,128)(2,1)S(1)}, u32[]{:S(2)}, u32[]{:S(2)}) collective-permute-start(bf16[16,2176]{1,0:T(8,128)(2,1)S(1)} %get-tuple-element.25), channel_id=1, source_target_pairs={{0,1},{1,0},{2,3},{3,2},{4,5},{5,4},{6,7},{7,6},{8,9},{9,8},{10,11... | collective-permute-start | bytes 208904 | tf_op jit(solution)/shard_map/ppermute | solution.py:278
  73.9 4.6 %collective-permute-start.12 = (bf16[16,2176]{1,0:T(8,128)(2,1)S(1)}, bf16[16,2176]{1,0:T(8,128)(2,1)S(1)}, u32[]{:S(2)}, u32[]{:S(2)}) collective-permute-start(bf16[16,2176]{1,0:T(8,128)(2,1)S(1)} %get-tuple-element.26), channel_id=1, source_target_pairs={{0,2},{1,3},{2,0},{3,1},{4,6},{5,7},{6,4},{7,5},{8,10},{9,11},{10,... | collective-permute-start | bytes 208904 | tf_op jit(solution)/shard_map/ppermute | solution.py:278
  75.9 5.2 %collective-permute-start.11 = (bf16[16,2176]{1,0:T(8,128)(2,1)S(1)}, bf16[16,2176]{1,0:T(8,128)(2,1)S(1)}, u32[]{:S(2)}, u32[]{:S(2)}) collective-permute-start(bf16[16,2176]{1,0:T(8,128)(2,1)S(1)} %get-tuple-element.27), channel_id=1, source_target_pairs={{0,3},{1,2},{2,1},{3,0},{4,7},{5,6},{6,5},{7,4},{8,11},{9,10},{10,... | collective-permute-start | bytes 208904 | tf_op jit(solution)/shard_map/ppermute | solution.py:278
  77.9 27.7 %copy-start.4 = (bf16[16,2176]{1,0:T(8,128)(2,1)}, bf16[16,2176]{1,0:T(8,128)(2,1)S(1)}, u32[]{:S(2)}) copy-start(bf16[16,2176]{1,0:T(8,128)(2,1)S(1)} %collective-permute-done.13.refs_6_) | copy-start | bytes 208900
  77.9 6.4 %collective-permute-start.10 = (bf16[16,2176]{1,0:T(8,128)(2,1)S(1)}, bf16[16,2176]{1,0:T(8,128)(2,1)S(1)}, u32[]{:S(2)}, u32[]{:S(2)}) collective-permute-start(bf16[16,2176]{1,0:T(8,128)(2,1)S(1)} %get-tuple-element.28), channel_id=1, source_target_pairs={{0,4},{1,5},{2,6},{3,7},{4,0},{5,1},{6,2},{7,3},{8,12},{9,13},{10,... | collective-permute-start | bytes 208904 | tf_op jit(solution)/shard_map/ppermute | solution.py:278
  78.5 27.2 %copy-start.5 = (bf16[16,2176]{1,0:T(8,128)(2,1)}, bf16[16,2176]{1,0:T(8,128)(2,1)S(1)}, u32[]{:S(2)}) copy-start(bf16[16,2176]{1,0:T(8,128)(2,1)S(1)} %collective-permute-done.12.refs_5_) | copy-start | bytes 208900
  78.5 29.2 %collective-permute-start.16 = (bf16[2,32,2176]{2,1,0:T(8,128)(2,1)}, bf16[2,32,2176]{2,1,0:T(8,128)(2,1)}, u32[]{:S(2)}, u32[]{:S(2)}) collective-permute-start(bf16[2,32,2176]{2,1,0:T(8,128)(2,1)} %collective-permute-done.14.refs_2_), channel_id=1, source_target_pairs={{0,8},{1,9},{2,10},{3,11},{4,12},{5,13},{6,14},{7,15},{8,0},{9,1},... | collective-permute-start | bytes 835592 | tf_op jit(solution)/shard_map/ppermute | solution.py:278
  81.1 24.5 %copy-start.6 = (bf16[16,2176]{1,0:T(8,128)(2,1)}, bf16[16,2176]{1,0:T(8,128)(2,1)S(1)}, u32[]{:S(2)}) copy-start(bf16[16,2176]{1,0:T(8,128)(2,1)S(1)} %collective-permute-done.11.refs_4_) | copy-start | bytes 208900
  81.1 26.5 %collective-permute-start.17 = (bf16[2,32,2176]{2,1,0:T(8,128)(2,1)}, bf16[2,32,2176]{2,1,0:T(8,128)(2,1)}, u32[]{:S(2)}, u32[]{:S(2)}) collective-permute-start(bf16[2,32,2176]{2,1,0:T(8,128)(2,1)} %collective-permute-done.15.refs_3_), channel_id=1, source_target_pairs={{0,8},{1,9},{2,10},{3,11},{4,12},{5,13},{6,14},{7,15},{8,0},{9,1},... | collective-permute-start | bytes 835592 | tf_op jit(solution)/shard_map/ppermute | solution.py:278
  84.3 20.7 %copy-start.7 = (bf16[16,2176]{1,0:T(8,128)(2,1)}, bf16[16,2176]{1,0:T(8,128)(2,1)S(1)}, u32[]{:S(2)}) copy-start(bf16[16,2176]{1,0:T(8,128)(2,1)S(1)} %collective-permute-done.10.refs_3_) | copy-start | bytes 208900
  84.3 7.0 %collective-permute-start.9 = (bf16[16,2176]{1,0:T(8,128)(2,1)S(1)}, bf16[16,2176]{1,0:T(8,128)(2,1)S(1)}, u32[]{:S(2)}, u32[]{:S(2)}) collective-permute-start(bf16[16,2176]{1,0:T(8,128)(2,1)S(1)} %get-tuple-element.29), channel_id=1, source_target_pairs={{0,5},{1,4},{2,7},{3,6},{4,1},{5,0},{6,3},{7,2},{8,13},{9,12},{10,... | collective-permute-start | bytes 208904 | tf_op jit(solution)/shard_map/ppermute | solution.py:278
  91.3 13.7 %copy-start.8 = (bf16[16,2176]{1,0:T(8,128)(2,1)}, bf16[16,2176]{1,0:T(8,128)(2,1)S(1)}, u32[]{:S(2)}) copy-start(bf16[16,2176]{1,0:T(8,128)(2,1)S(1)} %collective-permute-done.9.refs_2_) | copy-start | bytes 208900
  91.3 6.7 %collective-permute-start.8 = (bf16[16,2176]{1,0:T(8,128)(2,1)S(1)}, bf16[16,2176]{1,0:T(8,128)(2,1)S(1)}, u32[]{:S(2)}, u32[]{:S(2)}) collective-permute-start(bf16[16,2176]{1,0:T(8,128)(2,1)S(1)} %get-tuple-element.30), channel_id=1, source_target_pairs={{0,6},{1,7},{2,4},{3,5},{4,2},{5,3},{6,0},{7,1},{8,14},{9,15},{10,... | collective-permute-start | bytes 208904 | tf_op jit(solution)/shard_map/ppermute | solution.py:278
  98.0 7.0 %copy-start.9 = (bf16[16,2176]{1,0:T(8,128)(2,1)}, bf16[16,2176]{1,0:T(8,128)(2,1)S(1)}, u32[]{:S(2)}) copy-start(bf16[16,2176]{1,0:T(8,128)(2,1)S(1)} %collective-permute-done.8.refs_1_) | copy-start | bytes 208900
  98.0 7.0 %collective-permute-start.7 = (bf16[16,2176]{1,0:T(8,128)(2,1)S(1)}, bf16[16,2176]{1,0:T(8,128)(2,1)S(1)}, u32[]{:S(2)}, u32[]{:S(2)}) collective-permute-start(bf16[16,2176]{1,0:T(8,128)(2,1)S(1)} %get-tuple-element.31), channel_id=1, source_target_pairs={{0,7},{1,6},{2,5},{3,4},{4,3},{5,2},{6,1},{7,0},{8,15},{9,14},{10,... | collective-permute-start | bytes 208904 | tf_op jit(solution)/shard_map/ppermute | solution.py:278
  105.0 0.6 copy-start.10
where the time goes:
time: 118 us
  waiting for transfers between devices  55.9 us (47%)
  Pallas kernels  26.6 us (23%)
  starting transfers between devices  18.8 us (16%)
  local copies, waits for them, and re-layouts  14.1 us (12%)
  other arithmetic  1.68 us (1%)
    ppermute x21, waiting for transfers between devices, move(): return lax.ppermute(value, ('dp', 'expert'), pairs)  55.9 us
    ppermute x21, starting transfers between devices, move(): return lax.ppermute(value, ('dp', 'expert'), pairs)  18.8 us
    unnamed x22, local copies, waits for them, and re-layouts  13.4 us
    pallas_call x1, Pallas kernels, layer(): pl.pallas_call(functools.partial(_weights_kernel, local=local, rows=rows,...  10.2 us
    pallas_call x1, Pallas kernels, layer(): pl.pallas_call(kernel, out_shape=(piece,) * pair, in_specs=[smem] + [vmem...  4.96 us
    pallas_call x1, Pallas kernels, layer(): pl.pallas_call(functools.partial(_hidden_kernel, own=own, rows=rows, top=...  4.75 us
    pallas_call x3, Pallas kernels, layer(): pl.pallas_call(_fetch_kernel, out_shape=jax.ShapeDtypeStruct((own, width,...  3.02 us
  transfers between devices with their start and end apart: 21, of which 12 were waited for; matrix products, arithmetic and copies ran while one was open for 1% of the time, Pallas kernels for 12%

commit v1 on v0

--- a/solution.py
+++ b/solution.py
@@ -11,11 +11,12 @@
 F32 = jnp.float32
 BF16 = jnp.bfloat16
 LANES = 128
-HELD = ((2, 3, 6, 7), (4, 5, 1, 0))
+HELD = ((2, 0, 4, 5), (1, 3, 6, 7))
 BLOCKS = 8
-KERNEL_VMEM = 30 * 1024 * 1024
-WIDE_VMEM = 48 * 1024 * 1024
-FETCH_VMEM = 12 * 1024 * 1024
+SPLIT = 4
+KERNEL_VMEM = 20 * 1024 * 1024
+WIDE_VMEM = 32 * 1024 * 1024
+FETCH_VMEM = 4 * 1024 * 1024
 
 
 def _contract(left, right, left_dim, right_dim):
@@ -64,11 +65,22 @@
     packet[:, 2 * width :] = meta.T.astype(BF16)
 
 
-def _fetch_kernel(place, source, target, sem):
-    own = target.shape[0]
-    copies = [
-        pltpu.make_async_copy(source.at[place[0] + j], target.at[j], sem.at[j]) for j in range(own)
-    ]
+def _pieces(size):
+    step = size // SPLIT
+    return [pl.ds(n * step, step) for n in range(SPLIT)]
+
+
+def _fetch_kernel(place, *refs, skip):
+    *sources, target, sem = refs
+    number, _, total = target.shape
+    ff = total // len(sources)
+    copies = []
+    for j in range(number):
+        for i, source in enumerate(sources):
+            for n, rows in enumerate(_pieces(target.shape[1])):
+                part = target.at[j, rows, pl.ds(i * ff, ff)]
+                whole = source.at[place[0] + skip + j, rows, :]
+                copies.append(pltpu.make_async_copy(whole, part, sem.at[i, j, n]))
     for copy in copies:
         copy.start()
     for copy in copies:
@@ -93,9 +105,11 @@
 
 
 def _hidden_kernel(place, *refs, own, rows, top, inputs, block):
-    sources, (wg, wu, wd) = refs[:inputs], refs[inputs : inputs + 3]
-    hidden, chosen, prob, packets, packet_sems, rows_x, rows_dy = refs[inputs + 3 :]
-    _, width, ff = wg.shape
+    sources, weights = refs[:inputs], refs[inputs:-7]
+    *wide, wd = weights
+    hidden, chosen, prob, packets, packet_sems, rows_x, rows_dy = refs[-7:]
+    chunk = own // len(wide)
+    _, width, ff = wd.shape
     if inputs == 1:
         arrivals = [pltpu.make_async_copy(sources[0], packets, packet_sems.at[0, 0])]
         arrivals[0].start()
@@ -106,16 +120,16 @@
     for copy in arrivals:
         copy.wait()
     meta_t = packets[:, 2 * width :].astype(F32).T
-    picks, weights = _select(meta_t, _order(packets.shape[0]), place[1], own, rows, top)
+    picks, scales = _select(meta_t, _order(packets.shape[0]), place[1], own, rows, top)
     for j in range(own):
         chosen[j * rows : (j + 1) * rows, :] = picks[j].astype(BF16)
     rows_x[...] = _contract(chosen[...], packets[:, :width], 1, 0).astype(BF16)
     rows_dy[...] = _contract(chosen[...], packets[:, width : 2 * width], 1, 0).astype(BF16)
     for j in range(own):
         at = slice(j * rows, (j + 1) * rows)
-        scale = jnp.sum(picks[j] * weights[j], axis=1, keepdims=True)
-        gate = _contract(rows_x[at, :], wg[j], 1, 0)
-        up = _contract(rows_x[at, :], wu[j], 1, 0)
+        scale = jnp.sum(picks[j] * scales[j], axis=1, keepdims=True)
+        both = _contract(rows_x[at, :], wide[j // chunk][j % chunk], 1, 0)
+        gate, up = both[:, :ff], both[:, ff:]
         back = _contract(rows_dy[at, :], wd[j], 1, 0)
         sigma = jax.nn.sigmoid(gate)
         silu = gate * sigma
@@ -130,12 +144,14 @@
         prob[j] = jnp.broadcast_to(spread, prob.shape[1:])
 
 
-def _return_kernel(place, hidden, chosen, prob, wg, wu, keep, send, rows_out, *, own, rows, block):
-    _, width, ff = wg.shape
+def _return_kernel(place, hidden, chosen, prob, *refs, own, rows, block):
+    wide = refs[: -2 if block is None else -3]
+    keep, rows_out = refs[len(wide)], refs[-1]
+    width, both = wide[0].shape[1:]
+    chunk = own // len(wide)
     for j in range(own):
         at = slice(j * rows, (j + 1) * rows)
-        back = _contract(hidden[at, :ff], wg[j], 1, 1)
-        back = back + _contract(hidden[at, ff : 2 * ff], wu[j], 1, 1)
+        back = _contract(hidden[at, :both], wide[j // chunk][j % chunk], 1, 1)
         rows_out[at, :] = back.astype(BF16)
     part = _contract(chosen[...], rows_out[...], 0, 0).astype(BF16)
     tokens = part.shape[0]
@@ -144,19 +160,21 @@
     for j in range(own):
         total = total + jnp.where(lane == place[1] + j, prob[j].T[:, :1], 0.0)
     total = total.astype(BF16)
-    if send is None:
-        for s in range(tokens // block):
-            at = slice(s * block, (s + 1) * block)
+    if block is None:
+        single = keep.shape[1]
+        for s in range(tokens // single):
+            at = slice(s * single, (s + 1) * single)
             keep[s, :, :width] = part[at]
             keep[s, :, width:] = total[at]
         return
-    first = place[0] == 0
+    first, send = place[0] == 0, refs[-2]
     for s in range(tokens // block):
         low = slice(s * block, s * block + block // 2)
         high = slice(s * block + block // 2, (s + 1) * block)
         for value, lanes in ((part, slice(0, width)), (total, slice(width, None))):
-            keep[s, :, lanes] = jnp.where(first, value[low], value[high])
-            send[s, :, lanes] = jnp.where(first, value[high], value[low])
+            to = place[3] ^ s
+            keep[to, :, lanes] = jnp.where(first, value[low], value[high])
+            send[to, :, lanes] = jnp.where(first, value[high], value[low])
 
 
 def _weights_kernel(place, *refs, local, rows, top, sets, halves, block, half, ff, inputs):
@@ -185,7 +203,7 @@
         number = BLOCKS // 2
         both = [
             [[(array, i) for i in range(number)] for array in near],
-            [[(far[2 * side + i % 2], i // 2) for i in range(number)] for side in range(2)],
+            [[(far[2 * side + i // 2], i % 2) for i in range(number)] for side in range(2)],
         ]
         for s, (width, index) in enumerate(((2 * half, place[2]), (half, place[3]))):
             at = pl.multiple_of(index * cols, cols)
@@ -230,11 +248,8 @@
         copy.wait()
 
 
-def _finish_kernel(ids_t, kept, *refs):
-    *others, token_grad, prob_grad_t = refs
-    total = kept[...].astype(F32)
-    for other in others:
-        total = total + other[...].astype(F32)
+def _finish_kernel(ids_t, back, token_grad, prob_grad_t):
+    total = jnp.sum(back[...].astype(F32), axis=0)
     width = token_grad.shape[1]
     token_grad[...] = total[:, :width].astype(BF16)
     score = total[:, width:].T
@@ -244,6 +259,10 @@
         for k in range(ids_t.shape[0])
     ]
     prob_grad_t[...] = jnp.concatenate(found, axis=0).astype(BF16)
+
+
+def _in_hbm(values):
+    return [pltpu.with_memory_space_constraint(value, pltpu.HBM) for value in values]
 
 
 def _cost(flops, nbytes):
@@ -323,32 +342,34 @@
                 axis=1,
             )
 
-        near = to_rank(chip, 2, 4)
-        side = to_rank(chip, 6, 1)
-        near_side = to_rank(near, 1, 1)
-        side_side = to_rank(side, 1, None)
-        last_block = jnp.where(first, side_side, chip)
-        far_a = to_chip(jnp.stack([slim(near), slim(side)]))
-        far_b = to_chip(jnp.stack([slim(near_side), slim(last_block)]))
-        held = jnp.stack([near, near_side, side, last_block])
+        near = to_rank(chip, 2, 1)
+        side = to_rank(chip, 4, 6)
+        near_side = jnp.where(first, chip, to_rank(near, None, 2))
+        side_side = to_rank(side, 1, 1)
+        far_a = to_chip(jnp.stack([slim(near), slim(near_side)]))
+        far_b = to_chip(jnp.stack([slim(side), slim(side_side)]))
+        held = jnp.stack([near, near_side, side, side_side])
         gathered = [held, to_core(held)]
     else:
         gathered = [lax.all_gather(packet, "expert", axis=0, tiled=True)]
 
-    place = jnp.stack([core * own, rank * local + core * own, core]).astype(jnp.int32)
-    mine = []
-    for weight in (w_gate, w_up, w_down):
-        mine.append(
-            pl.pallas_call(
-                _fetch_kernel,
-                out_shape=jax.ShapeDtypeStruct((own, width, ff), BF16),
-                in_specs=[smem, hbm],
-                out_specs=vmem,
-                scratch_shapes=[pltpu.SemaphoreType.DMA((own,))],
-                compiler_params=pltpu.CompilerParams(vmem_limit_bytes=FETCH_VMEM),
-                cost_estimate=_cost(width * ff * own, 4 * own * width * ff),
-            )(place, weight)
-        )
+    place = jnp.stack([core * own, rank * local + core * own, core, rank]).astype(jnp.int32)
+
+    def fetch(weights, skip, number):
+        shape = (number, width, len(weights) * ff)
+        return pl.pallas_call(
+            functools.partial(_fetch_kernel, skip=skip),
+            out_shape=pltpu.VMEM(shape, BF16),
+            in_specs=[smem] + [hbm] * len(weights),
+            out_specs=vmem,
+            scratch_shapes=[pltpu.SemaphoreType.DMA((len(weights), number, SPLIT))],
+            compiler_params=pltpu.CompilerParams(vmem_limit_bytes=FETCH_VMEM),
+            cost_estimate=_cost(width * ff * own, 4 * own * width * ff),
+        )(place, *_in_hbm(weights))
+
+    chunk = own // pair
+    wide = [fetch((w_gate, w_up), i * chunk, chunk) for i in range(own // chunk)]
+    down = fetch((w_down,), 0, own)
     block = pair * tok_rows
     hidden, chosen, prob = pl.pallas_call(
         functools.partial(
@@ -359,7 +380,7 @@
             jax.ShapeDtypeStruct((own * rows, count), BF16),
             jax.ShapeDtypeStruct((own, 8, count), F32),
         ),
-        in_specs=[smem] + [hbm] * len(gathered) + [vmem] * 3,
+        in_specs=[smem] + [hbm] * len(gathered) + [vmem] * (len(wide) + 1),
         out_specs=(vmem, vmem, vmem),
         scratch_shapes=[
             pltpu.VMEM((count, 2 * width + LANES), BF16),
@@ -369,7 +390,7 @@
         compiler_params=limit,
         cost_estimate=_cost(6 * own * rows * width * ff, 6 * own * width * ff),
         name="hidden",
-    )(place, *gathered, *mine)
+    )(place, *gathered, *wide, down)
 
     if paired:
         sources = gathered + [far_a, far_b, to_core(far_a), to_core(far_b)]
@@ -384,31 +405,27 @@
         spread = lax.all_gather(hidden, "dp", axis=0)
         hidden_all = [spread[s] for s in range(sets)]
 
-    kernel = functools.partial(_return_kernel, own=own, rows=rows, block=block)
-    if pair == 1:
-        kernel = functools.partial(
-            lambda *refs, call: call(*refs[:7], None, *refs[7:]), call=kernel
-        )
+    kernel = functools.partial(
+        _return_kernel, own=own, rows=rows, block=block if paired else None
+    )
     piece = jax.ShapeDtypeStruct((ranks, tok_rows, width + extra), BF16)
     parts = pl.pallas_call(
         kernel,
         out_shape=(piece,) * pair,
-        in_specs=[smem] + [vmem] * 5,
+        in_specs=[smem] + [vmem] * (3 + len(wide)),
         out_specs=(vmem,) * pair,
         scratch_shapes=[pltpu.VMEM((own * rows, width), BF16)],
         compiler_params=limit,
         cost_estimate=_cost(8 * own * rows * width * ff, 4 * own * width * ff),
         name="contributions",
-    )(place, hidden, chosen, prob, *mine[:2])
+    )(place, hidden, chosen, prob, *wide)
 
     if paired:
         theirs = to_core(parts[1])
         summed = (parts[0].astype(F32) + theirs.astype(F32)).astype(BF16)
-        back = [summed[0]]
-        back += [to_rank(summed[i], i, i) for i in range(ranks - 1, 0, -1)]
     else:
-        back = lax.all_to_all(parts[0], "expert", 0, 0, tiled=True)
-        back = [back[i] for i in range(ranks)]
+        summed = parts[0]
+    back = lax.all_to_all(summed, "expert", 0, 0, tiled=True)
     place_all = jnp.stack([core * own, rank * local, dp, core]).astype(jnp.int32)
     shape = jax.ShapeDtypeStruct((local, cols, ff), F32)
     hidden_all = [value.reshape(own, rows, 3 * ff) for value in hidden_all]
@@ -447,10 +464,10 @@
             jax.ShapeDtypeStruct((tok_rows, width), BF16),
             jax.ShapeDtypeStruct((top, tok_rows), BF16),
         ),
-        in_specs=[vmem] * (1 + len(back)),
+        in_specs=[vmem] * 2,
         out_specs=(vmem, vmem),
         name="finish",
-    )(expert_ids.T, *back)
+    )(expert_ids.T, back)
     prob_grad = prob_grad_t.T
     return (token_grad, prob_grad, gate_grad, up_grad, down_grad)
 

time: 118 us -> 94.2 us (0.80)
  waiting for transfers between devices: 55.9 us -> 32.1 us
  local copies, waits for them, and re-layouts: 14.1 us -> 0.07 us
  Pallas kernels: 26.6 us -> 33.9 us
  starting transfers between devices: 18.8 us -> 22.2 us
  other arithmetic: 1.68 us -> 4.77 us
    ppermute x21 -> x14, waiting for transfers between devices: 55.9 us -> 32.1 us  [move(): return lax.ppermute(value, ('dp', 'expert'), pairs)]
    unnamed x22 -> x2, local copies, waits for them, and re-layouts: 13.4 us -> 0.01 us
    pallas_call x3, Pallas kernels: 3.02 us -> 10.4 us  [fetch(): pl.pallas_call(functools.partial(_fetch_kernel, skip=skip), out_shape=plt...]
    all_to_all x0 -> x1, starting transfers between devices: none -> 4.85 us  [layer(): back = lax.all_to_all(summed, 'expert', 0, 0, tiled=True)]
    another operation x8, other arithmetic: 0.35 us -> 2.62 us  [the longest x3 1.62 us: layer(): far_b = to_chip(jnp.stack([slim(side), slim(side_side)]))]
    ppermute x21 -> x14, starting transfers between devices: 18.8 us -> 17.3 us  [move(): return lax.ppermute(value, ('dp', 'expert'), pairs)]
  transfers between devices with their start and end apart: 21 -> 15, of which waited for: 12 -> 7; matrix products, arithmetic and copies ran while one was open for 1% -> 4% of each run, Pallas kernels for 12% -> 22%
where the time goes in v1:
time: 94.2 us; the launch traced here: 93.9 us
  Pallas kernels  33.9 us (36%)
  waiting for transfers between devices  32.1 us (34%)
  starting transfers between devices  22.2 us (24%)
  other arithmetic  4.77 us (5%)
    ppermute x14, waiting for transfers between devices, move(): return lax.ppermute(value, ('dp', 'expert'), pairs)  32.1 us
    ppermute x14, starting transfers between devices, move(): return lax.ppermute(value, ('dp', 'expert'), pairs)  17.3 us
    pallas_call x3, Pallas kernels, fetch(): pl.pallas_call(functools.partial(_fetch_kernel, skip=skip), out_shape=plt...  10.4 us
    pallas_call x1, Pallas kernels, layer(): pl.pallas_call(functools.partial(_weights_kernel, local=local, rows=rows,...  9.99 us
    pallas_call x1, Pallas kernels, layer(): pl.pallas_call(functools.partial(_hidden_kernel, own=own, rows=rows, top=...  5.23 us
    all_to_all x1, starting transfers between devices, layer(): back = lax.all_to_all(summed, 'expert', 0, 0, tiled=True)  4.85 us
    pallas_call x1, Pallas kernels, layer(): pl.pallas_call(kernel, out_shape=(piece,) * pair, in_specs=[smem] + [vmem...  4.76 us
    pallas_call x1, Pallas kernels, layer(): pl.pallas_call(_finish_kernel, out_shape=(jax.ShapeDtypeStruct((tok_rows,...  1.95 us
  transfers between devices with their start and end apart: 15, of which 7 were waited for; matrix products, arithmetic and copies ran while one was open for 4% of the time, Pallas kernels for 22%

profile of v1, /device:TPU:0, one launch (start us, length us, event | category | flops | bytes accessed | tf_op | source)
XLA Modules:
  0.0 93.9 jit_solution(9525082556009671943)
XLA Ops:
  0.6 1.6 %pack.1 = bf16[16,4224]{1,0:T(8,128)(2,1)} custom-call(bf16[16,2048]{1,0:T(8,128)(2,1)} %tokens.1, bf16[16,2048]{1,0:T(8,128)(2,1)} %out_grad.1, s32[8,16]{1,0:T(8,128)} %bitcast.32, bf16[8,16]{1,0:T(8,128)(2,1)} %bitcast.34), custom_call_target="tpu_custom_call" | custom-call | tf_op jit(solution)/shard_map/pack/pallas_call | solution.py:318
  2.2 0.5 collective-permute-start
  2.7 1.2 %collective-permute-done = bf16[16,4224]{1,0:T(8,128)(2,1)S(1)} collective-permute-done((bf16[16,4224]{1,0:T(8,128)(2,1)}, bf16[16,4224]{1,0:T(8,128)(2,1)S(1)}, u32[]{:S(2)}, u32[]{:S(2)}) %collective-permute-start) | collective-permute-done | bytes 135200 | tf_op jit(solution)/shard_map/ppermute | solution.py:297
  3.9 1.0 %maximum_select_fusion = bf16[32,4224]{1,0:T(8,128)(2,1)S(1)} fusion(bf16[16,4224]{1,0:T(8,128)(2,1)S(1)} %collective-permute-done, bf16[16,4224]{1,0:T(8,128)(2,1)} %pack.1, pred[]{:T(512)S(6)} %eq.3), kind=kLoop, calls=%fused_computation.4 | loop fusion | flops 1216512 | bytes 540673 | tf_op jit(solution)/shard_map/jit(_where)/select_n | solution.py:328
  5.0 3.0 %collective-permute-start.1 = (bf16[32,4224]{1,0:T(8,128)(2,1)S(1)}, bf16[32,4224]{1,0:T(8,128)(2,1)S(1)}, u32[]{:S(2)}, u32[]{:S(2)}) collective-permute-start(bf16[32,4224]{1,0:T(8,128)(2,1)S(1)} %maximum_select_fusion), channel_id=1, source_target_pairs={{0,2},{1,3},{2,0},{3,1},{4,6},{5,7},{6,4},{7,5},{8,9},{9,8},{10,11... | collective-permute-start | bytes 811016 | tf_op jit(solution)/shard_map/ppermute | solution.py:297
  8.0 2.6 %collective-permute-start.3 = (bf16[32,4224]{1,0:T(8,128)(2,1)S(1)}, bf16[32,4224]{1,0:T(8,128)(2,1)S(1)}, u32[]{:S(2)}, u32[]{:S(2)}) collective-permute-start(bf16[32,4224]{1,0:T(8,128)(2,1)S(1)} %maximum_select_fusion), channel_id=1, source_target_pairs={{0,4},{1,5},{2,6},{3,7},{4,0},{5,1},{6,2},{7,3},{8,14},{9,15},{10,... | collective-permute-start | bytes 811016 | tf_op jit(solution)/shard_map/ppermute | solution.py:297
  10.6 2.0 %collective-permute-done.1 = bf16[32,4224]{1,0:T(8,128)(2,1)S(1)} collective-permute-done((bf16[32,4224]{1,0:T(8,128)(2,1)S(1)}, bf16[32,4224]{1,0:T(8,128)(2,1)S(1)}, u32[]{:S(2)}, u32[]{:S(2)}) %collective-permute-start.1) | collective-permute-done | bytes 270368 | tf_op jit(solution)/shard_map/ppermute | solution.py:297
  12.5 0.7 collective-permute-start.2
  13.2 0.1 pad_add_fusion.place
  13.3 3.5 %shard_map.111.refs_3_.refs_1_ = bf16[2,2048,768]{2,1,0:T(8,128)(2,1)S(1)} custom-call(s32[4]{0:T(128)S(1)} %pad_add_fusion.place, bf16[8,2048,384]{2,1,0:T(8,128)(2,1)} %refs_0_.4, bf16[8,2048,384]{2,1,0:T(8,128)(2,1)} %refs_1_.3), custom_call_target="tpu_custom_call" | custom-call | flops 3145728 | bytes 12582912 | tf_op jit(solution)/shard_map/pallas_call | solution.py:360
  16.7 3.5 %shard_map.110.refs_2_.refs_0_ = bf16[2,2048,768]{2,1,0:T(8,128)(2,1)S(1)} custom-call(s32[4]{0:T(128)S(1)} %pad_add_fusion.place, bf16[8,2048,384]{2,1,0:T(8,128)(2,1)} %refs_0_.4, bf16[8,2048,384]{2,1,0:T(8,128)(2,1)} %refs_1_.3), custom_call_target="tpu_custom_call" | custom-call | flops 3145728 | bytes 12582912 | tf_op jit(solution)/shard_map/pallas_call | solution.py:360
  20.2 0.0 copy-start
  20.2 3.5 %shard_map.112.refs_4_ = bf16[4,2048,384]{2,1,0:T(8,128)(2,1)S(1)} custom-call(s32[4]{0:T(128)S(1)} %pad_add_fusion.place, bf16[8,2048,384]{2,1,0:T(8,128)(2,1)} %refs_0_.5), custom_call_target="tpu_custom_call" | custom-call | flops 3145728 | bytes 12582912 | tf_op jit(solution)/shard_map/pallas_call | solution.py:360
  23.7 0.0 collective-permute-done.3
  23.7 6.5 %collective-permute-start.4 = (bf16[32,4224]{1,0:T(8,128)(2,1)S(1)}, bf16[32,4224]{1,0:T(8,128)(2,1)S(1)}, u32[]{:S(2)}, u32[]{:S(2)}) collective-permute-start(bf16[32,4224]{1,0:T(8,128)(2,1)S(1)} %collective-permute-done.3), channel_id=1, source_target_pairs={{0,1},{1,0},{2,3},{3,2},{4,5},{5,4},{6,7},{7,6},{8,9},{9,8},{10,11... | collective-permute-start | bytes 811016 | tf_op jit(solution)/shard_map/ppermute | solution.py:297
  30.2 0.0 collective-permute-done.2
  30.2 0.0 copy-done
  30.2 0.1 broadcast_select_fusion
  30.3 4.3 %collective-permute-done.4 = bf16[32,4224]{1,0:T(8,128)(2,1)S(1)} collective-permute-done((bf16[32,4224]{1,0:T(8,128)(2,1)S(1)}, bf16[32,4224]{1,0:T(8,128)(2,1)S(1)}, u32[]{:S(2)}, u32[]{:S(2)}) %collective-permute-start.4) | collective-permute-done | bytes 270368 | tf_op jit(solution)/shard_map/ppermute | solution.py:297
  34.6 0.2 pad_maximum_fusion.refs_0_
  34.8 0.1 collective-permute-start.5
  34.9 2.6 %collective-permute-done.5.refs_1_ = bf16[4,32,4224]{2,1,0:T(8,128)(2,1)S(1)} collective-permute-done((bf16[4,32,4224]{2,1,0:T(8,128)(2,1)S(1)}, bf16[4,32,4224]{2,1,0:T(8,128)(2,1)S(1)}, u32[]{:S(2)}, u32[]{:S(2)}) %collective-permute-start.5) | collective-permute-done | bytes 1081376 | tf_op jit(solution)/shard_map/ppermute | solution.py:297
  37.5 5.2 %hidden.1 = (bf16[256,1152]{1,0:T(8,128)(2,1)S(1)}, bf16[256,256]{1,0:T(8,128)(2,1)S(1)}, f32[4,8,256]{2,1,0:T(8,128)S(1)}) custom-call(s32[4]{0:T(128)S(1)} %pad_add_fusion.place, bf16[4,32,4224]{2,1,0:T(8,128)(2,1)S(1)} %pad_maximum_fusion.refs_0_, bf16[4,32,4224]{2,1,0:T(8,128)(2,1)S(1)} %collective-permute-done.5.refs_1_, ...), custom_call_target="tpu_custom_call" | custom-call | flops 1207959552 | bytes 18874368 | tf_op jit(solution)/shard_map/hidden/pallas_call | solution.py:374
  42.8 4.8 %contributions.1 = (bf16[8,16,2176]{2,1,0:T(8,128)(2,1)S(1)}, bf16[8,16,2176]{2,1,0:T(8,128)(2,1)S(1)}) custom-call(s32[4]{0:T(128)S(1)} %pad_add_fusion.place, bf16[256,1152]{1,0:T(8,128)(2,1)S(1)} %get-tuple-element.15.hidden, bf16[256,256]{1,0:T(8,128)(2,1)S(1)} %get-tuple-element.16.chosen, f32[4,8,256]{2,1,0:T(8,128)S(1)} %get-tuple-element.17.prob, ...), custom_call_target="tpu_custom_call" | custom-call | flops 1610612736 | bytes 12582912 | tf_op jit(solution)/shard_map/contributions/pallas_call | solution.py:412
  47.5 0.2 collective-permute-start.6
  47.8 0.7 pad_maximum_fusion.1
  48.5 1.5 %collective-permute-start.7 = (bf16[2,32,2176]{2,1,0:T(8,128)(2,1)}, bf16[2,32,2176]{2,1,0:T(8,128)(2,1)}, u32[]{:S(2)}, u32[]{:S(2)}) collective-permute-start(bf16[2,32,2176]{2,1,0:T(8,128)(2,1)} %pad_maximum_fusion.1), channel_id=1, source_target_pairs={{0,16},{1,17},{2,18},{3,19},{4,20},{5,21},{6,22},{7,23},{8,24},{9,... | collective-permute-start | bytes 835592 | tf_op jit(solution)/shard_map/ppermute | solution.py:297
  50.0 0.7 maximum_bitcast_fusion.3
  50.7 0.6 collective-permute-start.12
  51.2 0.0 collective-permute-start.11
  51.2 0.0 collective-permute-done.6
  51.2 1.0 %add_convert_fusion = bf16[8,16,2176]{2,1,0:T(8,128)(2,1)} fusion(bf16[8,16,2176]{2,1,0:T(8,128)(2,1)S(1)} %collective-permute-done.6, bf16[8,16,2176]{2,1,0:T(8,128)(2,1)S(1)} %get-tuple-element.18), kind=kLoop, calls=%fused_computation | loop fusion | flops 1114112 | bytes 1671168 | tf_op jit(solution)/shard_map/convert_element_type | solution.py:425
  52.2 4.9 %all-to-all-start = ((bf16[8,16,2176]{2,1,0:T(8,128)(2,1)}), bf16[8,16,2176]{2,1,0:T(8,128)(2,1)}, u32[]{:S(2)}, u32[]{:S(2)}) async-start(bf16[8,16,2176]{2,1,0:T(8,128)(2,1)} %add_convert_fusion), calls=%async_computation | async-start | bytes 1114112 | tf_op jit(solution)/shard_map/all_to_all | solution.py:428
  57.0 13.2 %collective-permute-done.12 = bf16[256,1152]{1,0:T(8,128)(2,1)S(1)} collective-permute-done((bf16[256,1152]{1,0:T(8,128)(2,1)S(1)}, bf16[256,1152]{1,0:T(8,128)(2,1)S(1)}, u32[]{:S(2)}, u32[]{:S(2)}) %collective-permute-start.12) | collective-permute-done | bytes 589856 | tf_op jit(solution)/shard_map/ppermute | solution.py:297
  70.3 0.0 collective-permute-start.13
  70.3 0.9 pad_maximum_fusion.2
  71.2 1.6 %collective-permute-start.8 = (bf16[2,32,2176]{2,1,0:T(8,128)(2,1)S(1)}, bf16[2,32,2176]{2,1,0:T(8,128)(2,1)S(1)}, u32[]{:S(2)}, u32[]{:S(2)}) collective-permute-start(bf16[2,32,2176]{2,1,0:T(8,128)(2,1)S(1)} %pad_maximum_fusion.2), channel_id=1, source_target_pairs={{0,16},{1,17},{2,18},{3,19},{4,20},{5,21},{6,22},{7,23},{8,24},{9,... | collective-permute-start | bytes 835592 | tf_op jit(solution)/shard_map/ppermute | solution.py:297
  72.8 0.0 collective-permute-done.7.refs_2_
  72.8 0.2 collective-permute-start.9
  73.0 7.3 %collective-permute-done.8.refs_3_ = bf16[2,32,2176]{2,1,0:T(8,128)(2,1)S(1)} collective-permute-done((bf16[2,32,2176]{2,1,0:T(8,128)(2,1)S(1)}, bf16[2,32,2176]{2,1,0:T(8,128)(2,1)S(1)}, u32[]{:S(2)}, u32[]{:S(2)}) %collective-permute-start.8) | collective-permute-done | bytes 278560 | tf_op jit(solution)/shard_map/ppermute | solution.py:297
  80.3 0.0 collective-permute-start.10
  80.3 0.1 pad_add_fusion.1.place
  80.4 0.0 collective-permute-done.9.refs_4_
  80.4 1.5 %collective-permute-done.10.refs_5_ = bf16[2,32,2176]{2,1,0:T(8,128)(2,1)S(1)} collective-permute-done((bf16[2,32,2176]{2,1,0:T(8,128)(2,1)S(1)}, bf16[2,32,2176]{2,1,0:T(8,128)(2,1)S(1)}, u32[]{:S(2)}, u32[]{:S(2)}) %collective-permute-start.10) | collective-permute-done | bytes 278560 | tf_op jit(solution)/shard_map/ppermute | solution.py:297
  81.9 0.0 collective-permute-done.11
  81.9 0.0 collective-permute-done.13
  81.9 10.0 %weight_grads.1 = (f32[8,512,384]{2,1,0:T(8,128)}, f32[8,512,384]{2,1,0:T(8,128)}, f32[8,512,384]{2,1,0:T(8,128)}) custom-call(s32[4]{0:T(128)S(1)} %pad_add_fusion.1.place, bf16[4,32,4224]{2,1,0:T(8,128)(2,1)S(1)} %pad_maximum_fusion.refs_0_, bf16[4,32,4224]{2,1,0:T(8,128)(2,1)S(1)} %collective-permute-done.5.refs_1_, ...), custom_call_target="tpu_custom_call" | custom-call | flops 1207959552 | bytes 18874368 | tf_op jit(solution)/shard_map/weight_grads/pallas_call | solution.py:432
  91.9 0.0 all-to-all-done.back
  91.9 1.9 %finish.1 = (bf16[16,2048]{1,0:T(8,128)(2,1)}, bf16[8,16]{1,0:T(8,128)(2,1)}) custom-call(s32[8,16]{1,0:T(8,128)} %bitcast.33, bf16[8,16,2176]{2,1,0:T(8,128)(2,1)} %all-to-all-done.back), custom_call_target="tpu_custom_call" | custom-call | tf_op jit(solution)/shard_map/finish/pallas_call | solution.py:461
  (11 shorter events, 0.1 us)
Async XLA Ops:
  2.2 1.7 %collective-permute-start = (bf16[16,4224]{1,0:T(8,128)(2,1)}, bf16[16,4224]{1,0:T(8,128)(2,1)S(1)}, u32[]{:S(2)}, u32[]{:S(2)}) collective-permute-start(bf16[16,4224]{1,0:T(8,128)(2,1)} %pack.1), channel_id=1, source_target_pairs={{0,8},{1,9},{2,10},{3,11},{4,12},{5,13},{6,14},{7,15},{8,0},{9,1},... | collective-permute-start | bytes 405512 | tf_op jit(solution)/shard_map/ppermute | solution.py:297
  5.0 7.5 %collective-permute-start.1 = (bf16[32,4224]{1,0:T(8,128)(2,1)S(1)}, bf16[32,4224]{1,0:T(8,128)(2,1)S(1)}, u32[]{:S(2)}, u32[]{:S(2)}) collective-permute-start(bf16[32,4224]{1,0:T(8,128)(2,1)S(1)} %maximum_select_fusion), channel_id=1, source_target_pairs={{0,2},{1,3},{2,0},{3,1},{4,6},{5,7},{6,4},{7,5},{8,9},{9,8},{10,11... | collective-permute-start | bytes 811016 | tf_op jit(solution)/shard_map/ppermute | solution.py:297
  8.0 15.7 %collective-permute-start.3 = (bf16[32,4224]{1,0:T(8,128)(2,1)S(1)}, bf16[32,4224]{1,0:T(8,128)(2,1)S(1)}, u32[]{:S(2)}, u32[]{:S(2)}) collective-permute-start(bf16[32,4224]{1,0:T(8,128)(2,1)S(1)} %maximum_select_fusion), channel_id=1, source_target_pairs={{0,4},{1,5},{2,6},{3,7},{4,0},{5,1},{6,2},{7,3},{8,14},{9,15},{10,... | collective-permute-start | bytes 811016 | tf_op jit(solution)/shard_map/ppermute | solution.py:297
  12.5 17.7 %collective-permute-start.2 = (bf16[32,4224]{1,0:T(8,128)(2,1)S(1)}, bf16[32,4224]{1,0:T(8,128)(2,1)S(1)}, u32[]{:S(2)}, u32[]{:S(2)}) collective-permute-start(bf16[32,4224]{1,0:T(8,128)(2,1)S(1)} %collective-permute-done.1), channel_id=1, source_target_pairs={{8,10},{9,11},{10,8},{11,9},{12,14},{13,15},{14,12},{15,13},{24,26... | collective-permute-start | bytes 811016 | tf_op jit(solution)/shard_map/ppermute | solution.py:297
  20.2 10.0 %copy-start = (bf16[16,4224]{1,0:T(8,128)(2,1)S(1)}, bf16[16,4224]{1,0:T(8,128)(2,1)}, u32[]{:S(2)}) copy-start(bf16[16,4224]{1,0:T(8,128)(2,1)} %pack.1) | copy-start | bytes 405508
  23.7 10.9 %collective-permute-start.4 = (bf16[32,4224]{1,0:T(8,128)(2,1)S(1)}, bf16[32,4224]{1,0:T(8,128)(2,1)S(1)}, u32[]{:S(2)}, u32[]{:S(2)}) collective-permute-start(bf16[32,4224]{1,0:T(8,128)(2,1)S(1)} %collective-permute-done.3), channel_id=1, source_target_pairs={{0,1},{1,0},{2,3},{3,2},{4,5},{5,4},{6,7},{7,6},{8,9},{9,8},{10,11... | collective-permute-start | bytes 811016 | tf_op jit(solution)/shard_map/ppermute | solution.py:297
  34.8 2.8 %collective-permute-start.5 = (bf16[4,32,4224]{2,1,0:T(8,128)(2,1)S(1)}, bf16[4,32,4224]{2,1,0:T(8,128)(2,1)S(1)}, u32[]{:S(2)}, u32[]{:S(2)}) collective-permute-start(bf16[4,32,4224]{2,1,0:T(8,128)(2,1)S(1)} %pad_maximum_fusion.refs_0_), channel_id=1, source_target_pairs={{0,8},{1,9},{2,10},{3,11},{4,12},{5,13},{6,14},{7,15},{8,0},{9,1},... | collective-permute-start | bytes 3244040 | tf_op jit(solution)/shard_map/ppermute | solution.py:297
  47.5 3.7 %collective-permute-start.6 = (bf16[8,16,2176]{2,1,0:T(8,128)(2,1)S(1)}, bf16[8,16,2176]{2,1,0:T(8,128)(2,1)S(1)}, u32[]{:S(2)}, u32[]{:S(2)}) collective-permute-start(bf16[8,16,2176]{2,1,0:T(8,128)(2,1)S(1)} %get-tuple-element.19), channel_id=1, source_target_pairs={{0,8},{1,9},{2,10},{3,11},{4,12},{5,13},{6,14},{7,15},{8,0},{9,1},... | collective-permute-start | bytes 1671176 | tf_op jit(solution)/shard_map/ppermute | solution.py:297
  48.5 24.3 %collective-permute-start.7 = (bf16[2,32,2176]{2,1,0:T(8,128)(2,1)}, bf16[2,32,2176]{2,1,0:T(8,128)(2,1)}, u32[]{:S(2)}, u32[]{:S(2)}) collective-permute-start(bf16[2,32,2176]{2,1,0:T(8,128)(2,1)} %pad_maximum_fusion.1), channel_id=1, source_target_pairs={{0,16},{1,17},{2,18},{3,19},{4,20},{5,21},{6,22},{7,23},{8,24},{9,... | collective-permute-start | bytes 835592 | tf_op jit(solution)/shard_map/ppermute | solution.py:297
  50.7 19.6 %collective-permute-start.12 = (bf16[256,1152]{1,0:T(8,128)(2,1)S(1)}, bf16[256,1152]{1,0:T(8,128)(2,1)S(1)}, u32[]{:S(2)}, u32[]{:S(2)}) collective-permute-start(bf16[256,1152]{1,0:T(8,128)(2,1)S(1)} %get-tuple-element.15.hidden), channel_id=1, source_target_pairs={{0,16},{1,17},{2,18},{3,19},{4,20},{5,21},{6,22},{7,23},{8,24},{9,... | collective-permute-start | bytes 1769480 | tf_op jit(solution)/shard_map/ppermute | solution.py:297
  51.2 30.7 %collective-permute-start.11 = (bf16[256,1152]{1,0:T(8,128)(2,1)S(1)}, bf16[256,1152]{1,0:T(8,128)(2,1)}, u32[]{:S(2)}, u32[]{:S(2)}) collective-permute-start(bf16[256,1152]{1,0:T(8,128)(2,1)S(1)} %get-tuple-element.15.hidden), channel_id=1, source_target_pairs={{0,8},{1,9},{2,10},{3,11},{4,12},{5,13},{6,14},{7,15},{8,0},{9,1},... | collective-permute-start | bytes 1769480 | tf_op jit(solution)/shard_map/ppermute | solution.py:297
  52.2 39.7 %all-to-all-start = ((bf16[8,16,2176]{2,1,0:T(8,128)(2,1)}), bf16[8,16,2176]{2,1,0:T(8,128)(2,1)}, u32[]{:S(2)}, u32[]{:S(2)}) async-start(bf16[8,16,2176]{2,1,0:T(8,128)(2,1)} %add_convert_fusion), calls=%async_computation | async-start | bytes 1114112 | tf_op jit(solution)/shard_map/all_to_all | solution.py:428
  70.3 11.6 %collective-permute-start.13 = (bf16[256,1152]{1,0:T(8,128)(2,1)S(1)}, bf16[256,1152]{1,0:T(8,128)(2,1)S(1)}, u32[]{:S(2)}, u32[]{:S(2)}) collective-permute-start(bf16[256,1152]{1,0:T(8,128)(2,1)S(1)} %collective-permute-done.12), channel_id=1, source_target_pairs={{0,8},{1,9},{2,10},{3,11},{4,12},{5,13},{6,14},{7,15},{8,0},{9,1},... | collective-permute-start | bytes 1769480 | tf_op jit(solution)/shard_map/ppermute | solution.py:297
  71.2 9.1 %collective-permute-start.8 = (bf16[2,32,2176]{2,1,0:T(8,128)(2,1)S(1)}, bf16[2,32,2176]{2,1,0:T(8,128)(2,1)S(1)}, u32[]{:S(2)}, u32[]{:S(2)}) collective-permute-start(bf16[2,32,2176]{2,1,0:T(8,128)(2,1)S(1)} %pad_maximum_fusion.2), channel_id=1, source_target_pairs={{0,16},{1,17},{2,18},{3,19},{4,20},{5,21},{6,22},{7,23},{8,24},{9,... | collective-permute-start | bytes 835592 | tf_op jit(solution)/shard_map/ppermute | solution.py:297
  72.8 7.7 %collective-permute-start.9 = (bf16[2,32,2176]{2,1,0:T(8,128)(2,1)}, bf16[2,32,2176]{2,1,0:T(8,128)(2,1)S(1)}, u32[]{:S(2)}, u32[]{:S(2)}) collective-permute-start(bf16[2,32,2176]{2,1,0:T(8,128)(2,1)} %collective-permute-done.7.refs_2_), channel_id=1, source_target_pairs={{0,8},{1,9},{2,10},{3,11},{4,12},{5,13},{6,14},{7,15},{8,0},{9,1},... | collective-permute-start | bytes 835592 | tf_op jit(solution)/shard_map/ppermute | solution.py:297
  80.3 1.6 %collective-permute-start.10 = (bf16[2,32,2176]{2,1,0:T(8,128)(2,1)S(1)}, bf16[2,32,2176]{2,1,0:T(8,128)(2,1)S(1)}, u32[]{:S(2)}, u32[]{:S(2)}) collective-permute-start(bf16[2,32,2176]{2,1,0:T(8,128)(2,1)S(1)} %collective-permute-done.8.refs_3_), channel_id=1, source_target_pairs={{0,8},{1,9},{2,10},{3,11},{4,12},{5,13},{6,14},{7,15},{8,0},{9,1},... | collective-permute-start | bytes 835592 | tf_op jit(solution)/shard_map/ppermute | solution.py:297

commit v2 on v1

--- a/solution.py
+++ b/solution.py
@@ -11,7 +11,6 @@
 F32 = jnp.float32
 BF16 = jnp.bfloat16
 LANES = 128
-HELD = ((2, 0, 4, 5), (1, 3, 6, 7))
 BLOCKS = 8
 SPLIT = 4
 KERNEL_VMEM = 20 * 1024 * 1024
@@ -87,20 +86,9 @@
         copy.wait()
 
 
-def _collect(core, sources, pieces, sems, block):
-    copies = []
-    for side, arrays in enumerate(sources):
-        for i in range(BLOCKS // 2):
-            array, index = arrays[i]
-            at = lax.select(core == side, HELD[0][i], HELD[1][i]) * block
-            rows = pl.ds(pl.multiple_of(at, block), block)
-            for n, (columns, target) in enumerate(pieces):
-                source = array.at[index, :, columns]
-                copy = pltpu.make_async_copy(
-                    source, target.at[rows, :], sems.at[n, side * (BLOCKS // 2) + i]
-                )
-                copy.start()
-                copies.append(copy)
+def _start(copies):
+    for copy in copies:
+        copy.start()
     return copies
 
 
@@ -111,20 +99,25 @@
     chunk = own // len(wide)
     _, width, ff = wd.shape
     if inputs == 1:
-        arrivals = [pltpu.make_async_copy(sources[0], packets, packet_sems.at[0, 0])]
-        arrivals[0].start()
+        whole = packets.at[:, 0]
+        arrivals = _start([pltpu.make_async_copy(sources[0], whole, packet_sems.at[0, 0])])
     else:
-        both = [[(array, i) for i in range(BLOCKS // 2)] for array in sources]
-        whole = [(slice(None), packets)]
-        arrivals = _collect(place[2], both, whole, packet_sems, block)
+        arrivals = _start(
+            [
+                pltpu.make_async_copy(array, packets.at[:, (place[2] + i) % 2], packet_sems.at[0, i])
+                for i, array in enumerate(sources)
+            ]
+        )
     for copy in arrivals:
         copy.wait()
-    meta_t = packets[:, 2 * width :].astype(F32).T
-    picks, scales = _select(meta_t, _order(packets.shape[0]), place[1], own, rows, top)
+    count = chosen.shape[1]
+    meta_t = packets[..., 2 * width :].reshape(count, LANES).astype(F32).T
+    picks, scales = _select(meta_t, _order(count), place[1], own, rows, top)
     for j in range(own):
         chosen[j * rows : (j + 1) * rows, :] = picks[j].astype(BF16)
-    rows_x[...] = _contract(chosen[...], packets[:, :width], 1, 0).astype(BF16)
-    rows_dy[...] = _contract(chosen[...], packets[:, width : 2 * width], 1, 0).astype(BF16)
+    rows_x[...] = _contract(chosen[...], packets[..., :width].reshape(count, width), 1, 0).astype(BF16)
+    grads = packets[..., width : 2 * width].reshape(count, width)
+    rows_dy[...] = _contract(chosen[...], grads, 1, 0).astype(BF16)
     for j in range(own):
         at = slice(j * rows, (j + 1) * rows)
         scale = jnp.sum(picks[j] * scales[j], axis=1, keepdims=True)
@@ -181,38 +174,35 @@
     sources, hidden = refs[:inputs], refs[inputs : inputs + sets * halves]
     rest = refs[inputs + sets * halves :]
     outs, (metas, xs, dys, sems, held, gate, up, down, in_sems, out_sems) = rest[:3], rest[3:]
-    count, cols = xs.shape[1:]
+    cols = xs.shape[-1]
+    count = xs.shape[1] * xs.shape[2] * xs.shape[3]
     per_half = local // halves
     copies = []
+    spans = []
     if inputs == sets:
         for s in range(sets):
-            for n, (columns, target) in enumerate(
-                (
-                    (slice(0, cols), xs),
-                    (slice(cols, 2 * cols), dys),
-                    (slice(2 * cols, None), metas),
-                )
-            ):
-                copy = pltpu.make_async_copy(
-                    sources[s].at[:, columns], target.at[s], sems.at[s, n, 0]
-                )
-                copy.start()
-                copies.append(copy)
+            spans.append((sources[s], s, slice(None), 0, 0, cols, 0))
     else:
         near, far = sources[:2], sources[2:]
-        number = BLOCKS // 2
-        both = [
-            [[(array, i) for i in range(number)] for array in near],
-            [[(far[2 * side + i // 2], i % 2) for i in range(number)] for side in range(2)],
-        ]
-        for s, (width, index) in enumerate(((2 * half, place[2]), (half, place[3]))):
-            at = pl.multiple_of(index * cols, cols)
-            pieces = (
-                (pl.ds(at, cols), xs.at[s]),
-                (pl.ds(pl.multiple_of(width + at, cols), cols), dys.at[s]),
-                (slice(2 * width, None), metas.at[s]),
-            )
-            copies += _collect(place[3], both[s], pieces, sems.at[s], block)
+        for i in range(2):
+            lane = (place[3] + i) % 2
+            at = pl.multiple_of(place[2] * cols, cols)
+            spans.append((near[i], 0, slice(None), lane, at, 2 * half, i))
+            at = pl.multiple_of(place[3] * cols, cols)
+            for part in range(2):
+                blocks = pl.ds(part * BLOCKS // 2, BLOCKS // 2)
+                spans.append((far[2 * i + part], 1, blocks, lane, at, half, 2 * i + part))
+    for source, s, blocks, lane, at, span, sem in spans:
+        pieces = (
+            (pl.ds(at, cols), xs),
+            (pl.ds(pl.multiple_of(span + at, cols), cols), dys),
+            (slice(2 * span, None), metas),
+        )
+        for n, (columns, target) in enumerate(pieces):
+            to = target.at[s, blocks, lane]
+            copy = pltpu.make_async_copy(source.at[:, :, columns], to, sems.at[s, n, sem])
+            copy.start()
+            copies.append(copy)
     for at_half in range(halves):
         for s in range(sets):
             target = held.at[pl.ds(at_half * per_half, per_half), pl.ds(s * rows, rows), :]
@@ -225,7 +215,7 @@
         copy.wait()
     picks = []
     for s in range(sets):
-        turned = metas[s].astype(F32).T
+        turned = metas[s].reshape(count, LANES).astype(F32).T
         picks.append(_select(turned, order, place[1], local, rows, top, place[0])[0])
     departures = []
     for j in range(local):
@@ -233,7 +223,7 @@
         turned = []
         for source in (xs, dys):
             taken = [
-                _contract(picks[s][j].astype(BF16), source[s], 1, 0).astype(BF16)
+                _contract(picks[s][j].astype(BF16), source[s].reshape(count, cols), 1, 0).astype(BF16)
                 for s in range(sets)
             ]
             turned.append(jnp.concatenate(taken, axis=0))
@@ -302,14 +292,8 @@
     def to_chip(value):
         return move(value, lambda d, e: (d ^ 2, e))
 
-    def to_rank(value, first, second):
-        def target(d, e):
-            off = second if d % 2 else first
-            return None if off is None else (d, e ^ off)
-
-        return move(value, target)
-
-    first = core == 0
+    def to_rank(value, offset):
+        return move(value, lambda d, e: (d, e ^ offset))
 
     vmem = pl.BlockSpec(memory_space=pltpu.VMEM)
     smem = pl.BlockSpec(memory_space=pltpu.SMEM)
@@ -324,34 +308,32 @@
     )(tokens, out_grad, expert_ids.T, probs.T)
     half = width // sets
     if paired:
-        other = to_core(packet)
-        chip = jnp.where(
-            first,
-            jnp.concatenate([packet, other], axis=0),
-            jnp.concatenate([other, packet], axis=0),
-        )
         at = (1 - dp // pair) * half
 
         def slim(block):
+            size = block.shape[:2] + (half,)
             return jnp.concatenate(
                 [
-                    lax.dynamic_slice(block, (0, at), (block.shape[0], half)),
-                    lax.dynamic_slice(block, (0, width + at), (block.shape[0], half)),
-                    block[:, 2 * width :],
+                    lax.dynamic_slice(block, (0, 0, at), size),
+                    lax.dynamic_slice(block, (0, 0, width + at), size),
+                    block[:, :, 2 * width :],
                 ],
-                axis=1,
+                axis=2,
             )
 
-        near = to_rank(chip, 2, 1)
-        side = to_rank(chip, 4, 6)
-        near_side = jnp.where(first, chip, to_rank(near, None, 2))
-        side_side = to_rank(side, 1, 1)
-        far_a = to_chip(jnp.stack([slim(near), slim(near_side)]))
-        far_b = to_chip(jnp.stack([slim(side), slim(side_side)]))
-        held = jnp.stack([near, near_side, side, side_side])
+        far_z = to_rank(packet, 6)
+        mid_z = to_rank(packet, 4)
+        low = jnp.stack([packet, to_rank(packet, 1)])
+        low = jnp.concatenate([low, to_rank(low, 2)])
+        high = jnp.stack([mid_z, far_z])
+        relay = to_rank(high, 1)
+        high = jnp.stack([high[0], relay[0], high[1], relay[1]])
+        far_a = to_chip(slim(low))
+        far_b = to_chip(slim(high))
+        held = jnp.concatenate([low, high])
         gathered = [held, to_core(held)]
     else:
-        gathered = [lax.all_gather(packet, "expert", axis=0, tiled=True)]
+        gathered = [lax.all_gather(packet, "expert", axis=0)]
 
     place = jnp.stack([core * own, rank * local + core * own, core, rank]).astype(jnp.int32)
 
@@ -383,8 +365,8 @@
         in_specs=[smem] + [hbm] * len(gathered) + [vmem] * (len(wide) + 1),
         out_specs=(vmem, vmem, vmem),
         scratch_shapes=[
-            pltpu.VMEM((count, 2 * width + LANES), BF16),
-            pltpu.SemaphoreType.DMA((1, BLOCKS)),
+            pltpu.VMEM((ranks, pair, tok_rows, 2 * width + LANES), BF16),
+            pltpu.SemaphoreType.DMA((1, 2)),
         ]
         + [pltpu.VMEM((own * rows, width), BF16)] * 2,
         compiler_params=limit,
@@ -397,11 +379,11 @@
         hidden_far = to_chip(hidden)
         hidden_all = [hidden, to_core(hidden), hidden_far, to_core(hidden_far)]
     else:
-        by_owner = gathered[0][:, : 2 * width].reshape(count, 2, groups, cols)
-        by_owner = jnp.moveaxis(by_owner, 2, 0).reshape(groups, count, 2 * cols)
+        by_owner = gathered[0][:, :, : 2 * width].reshape(ranks, tok_rows, 2, groups, cols)
+        by_owner = jnp.moveaxis(by_owner, 3, 0).reshape(groups, ranks, tok_rows, 2 * cols)
         moved = lax.all_to_all(by_owner, "dp", 0, 0, tiled=True)
-        metas = lax.all_gather(gathered[0][:, 2 * width :], "dp", axis=0)
-        sources = [jnp.concatenate([moved[s], metas[s]], axis=1) for s in range(sets)]
+        metas = lax.all_gather(gathered[0][:, :, 2 * width :], "dp", axis=0)
+        sources = [jnp.concatenate([moved[s], metas[s]], axis=2) for s in range(sets)]
         spread = lax.all_gather(hidden, "dp", axis=0)
         hidden_all = [spread[s] for s in range(sets)]
 
@@ -446,10 +428,10 @@
         in_specs=[smem] + [hbm] * (len(sources) + len(hidden_all)),
         out_specs=(hbm, hbm, hbm),
         scratch_shapes=[
-            pltpu.VMEM((sets, count, LANES), BF16),
-            pltpu.VMEM((sets, count, cols), BF16),
-            pltpu.VMEM((sets, count, cols), BF16),
-            pltpu.SemaphoreType.DMA((sets, 3, BLOCKS)),
+            pltpu.VMEM((sets, ranks, pair, tok_rows, LANES), BF16),
+            pltpu.VMEM((sets, ranks, pair, tok_rows, cols), BF16),
+            pltpu.VMEM((sets, ranks, pair, tok_rows, cols), BF16),
+            pltpu.SemaphoreType.DMA((sets, 3, 4)),
             pltpu.VMEM((local, sets * rows, 3 * ff), BF16),
         ]
         + [pltpu.VMEM((local, cols, ff), F32)] * 3

time: 94.2 us -> 91.8 us (0.975)
  starting transfers between devices: 22.2 us -> 15.8 us
  waiting for transfers between devices: 32.1 us -> 35.9 us
  local copies, waits for them, and re-layouts: 0.07 us -> 1.9 us
    ppermute x14, starting transfers between devices: 17.3 us -> 11.5 us  [move(): return lax.ppermute(value, ('dp', 'expert'), pairs)]
    ppermute x14, waiting for transfers between devices: 32.1 us -> 35.9 us  [move(): return lax.ppermute(value, ('dp', 'expert'), pairs)]
    concatenate x0 -> x3, other arithmetic: none -> 1.72 us  [the longest x2 1.66 us: slim(): jnp.concatenate([lax.dynamic_slice(block, (0, 0, at), size), lax.dynamic_...]
    another operation x7 -> x3, other arithmetic: 2.55 us -> 1.05 us  [the longest x1 0.94 us: layer(): low = jnp.stack([packet, to_rank(packet, 1)])]
    select_n x2 -> x0, other arithmetic: 1.12 us -> none  [the longest x1 1.04 us: layer(): jnp.where(first, jnp.concatenate([packet, other], axis=0), jnp.concatenat...]
    unnamed x2 -> x9, local copies, waits for them, and re-layouts: 0.01 us -> 1.04 us
  transfers between devices with their start and end apart: 15 -> 15, of which waited for: 7 -> 7; matrix products, arithmetic and copies ran while one was open for 4% -> 6% of each run, Pallas kernels for 22% -> 32%
where the time goes in v2:
time: 91.8 us; the launch traced here: 91.5 us
  waiting for transfers between devices  35.9 us (39%)
  Pallas kernels  33.2 us (36%)
  starting transfers between devices  15.8 us (17%)
  other arithmetic  3.87 us (4%)
  local copies, waits for them, and re-layouts  1.9 us (2%)
    ppermute x14, waiting for transfers between devices, move(): return lax.ppermute(value, ('dp', 'expert'), pairs)  35.9 us
    ppermute x14, starting transfers between devices, move(): return lax.ppermute(value, ('dp', 'expert'), pairs)  11.5 us
    pallas_call x3, Pallas kernels, fetch(): pl.pallas_call(functools.partial(_fetch_kernel, skip=skip), out_shape=plt...  10.4 us
    pallas_call x1, Pallas kernels, layer(): pl.pallas_call(functools.partial(_weights_kernel, local=local, rows=rows,...  9.54 us
    pallas_call x1, Pallas kernels, layer(): pl.pallas_call(functools.partial(_hidden_kernel, own=own, rows=rows, top=...  4.97 us
    pallas_call x1, Pallas kernels, layer(): pl.pallas_call(kernel, out_shape=(piece,) * pair, in_specs=[smem] + [vmem...  4.76 us
    all_to_all x1, starting transfers between devices, layer(): back = lax.all_to_all(summed, 'expert', 0, 0, tiled=True)  4.37 us
    pallas_call x1, Pallas kernels, layer(): pl.pallas_call(_finish_kernel, out_shape=(jax.ShapeDtypeStruct((tok_rows,...  1.95 us
  transfers between devices with their start and end apart: 15, of which 7 were waited for; matrix products, arithmetic and copies ran while one was open for 6% of the time, Pallas kernels for 32%

profile of v2, /device:TPU:0, one launch (start us, length us, event | category | flops | bytes accessed | tf_op | source)
XLA Modules:
  0.0 91.5 jit_solution(2895157111766274162)
XLA Ops:
  0.6 1.6 %pack.1 = bf16[16,4224]{1,0:T(8,128)(2,1)} custom-call(bf16[16,2048]{1,0:T(8,128)(2,1)} %tokens.1, bf16[16,2048]{1,0:T(8,128)(2,1)} %out_grad.1, s32[8,16]{1,0:T(8,128)} %bitcast.32, bf16[8,16]{1,0:T(8,128)(2,1)} %bitcast.34), custom_call_target="tpu_custom_call" | custom-call | tf_op jit(solution)/shard_map/pack/pallas_call | solution.py:302
  2.2 5.1 %collective-permute-start.3 = (bf16[16,4224]{1,0:T(8,128)(2,1)}, bf16[16,4224]{1,0:T(8,128)(2,1)S(1)}, u32[]{:S(2)}, u32[]{:S(2)}) collective-permute-start(bf16[16,4224]{1,0:T(8,128)(2,1)} %pack.1), channel_id=1, source_target_pairs={{0,6},{1,7},{2,4},{3,5},{4,2},{5,3},{6,0},{7,1},{8,14},{9,15},{10,... | collective-permute-start | bytes 405512 | tf_op jit(solution)/shard_map/ppermute | solution.py:287
  7.3 0.0 collective-permute-start.2
  7.3 1.5 %collective-permute-start = (bf16[16,4224]{1,0:T(8,128)(2,1)}, bf16[16,4224]{1,0:T(8,128)(2,1)S(1)}, u32[]{:S(2)}, u32[]{:S(2)}) collective-permute-start(bf16[16,4224]{1,0:T(8,128)(2,1)} %pack.1), channel_id=1, source_target_pairs={{0,1},{1,0},{2,3},{3,2},{4,5},{5,4},{6,7},{7,6},{8,9},{9,8},{10,11... | collective-permute-start | bytes 405512 | tf_op jit(solution)/shard_map/ppermute | solution.py:287
  8.8 0.9 %constant_dynamic-update-slice_fusion.6 = bf16[8,16,4224]{2,1,0:T(8,128)(2,1)S(1)} fusion(bf16[16,4224]{1,0:T(8,128)(2,1)} %pack.1), kind=kLoop, calls=%fused_computation.13 | loop fusion | bytes 270336
  9.8 2.3 %collective-permute-done.3 = bf16[16,4224]{1,0:T(8,128)(2,1)S(1)} collective-permute-done((bf16[16,4224]{1,0:T(8,128)(2,1)}, bf16[16,4224]{1,0:T(8,128)(2,1)S(1)}, u32[]{:S(2)}, u32[]{:S(2)}) %collective-permute-start.3) | collective-permute-done | bytes 135200 | tf_op jit(solution)/shard_map/ppermute | solution.py:287
  12.1 6.9 %collective-permute-done.2 = bf16[16,4224]{1,0:T(8,128)(2,1)S(1)} collective-permute-done((bf16[16,4224]{1,0:T(8,128)(2,1)}, bf16[16,4224]{1,0:T(8,128)(2,1)S(1)}, u32[]{:S(2)}, u32[]{:S(2)}) %collective-permute-start.2) | collective-permute-done | bytes 135200 | tf_op jit(solution)/shard_map/ppermute | solution.py:287
  19.0 1.6 %collective-permute-start.4 = (bf16[2,16,4224]{2,1,0:T(8,128)(2,1)S(1)}, bf16[2,16,4224]{2,1,0:T(8,128)(2,1)S(1)}, u32[]{:S(2)}, u32[]{:S(2)}) collective-permute-start(bf16[2,16,4224]{2,1,0:T(8,128)(2,1)S(1)} %pad_maximum_fusion.5), channel_id=1, source_target_pairs={{0,1},{1,0},{2,3},{3,2},{4,5},{5,4},{6,7},{7,6},{8,9},{9,8},{10,11... | collective-permute-start | bytes 811016 | tf_op jit(solution)/shard_map/ppermute | solution.py:287
  20.6 0.0 collective-permute-done
  20.6 0.9 %pad_maximum_fusion.4 = bf16[2,16,4224]{2,1,0:T(8,128)(2,1)S(1)} fusion(bf16[1,16,4224]{2,1,0:T(8,128)(2,1)S(1)} %bitcast.30, bf16[1,16,4224]{2,1,0:T(8,128)(2,1)} %bitcast.24), kind=kLoop, calls=%fused_computation.5 | loop fusion | flops 135168 | bytes 540672 | tf_op jit(solution)/shard_map/stack | solution.py:326
  21.5 0.1 collective-permute-start.1
  21.6 7.2 %collective-permute-done.1 = bf16[2,16,4224]{2,1,0:T(8,128)(2,1)S(1)} collective-permute-done((bf16[2,16,4224]{2,1,0:T(8,128)(2,1)S(1)}, bf16[2,16,4224]{2,1,0:T(8,128)(2,1)S(1)}, u32[]{:S(2)}, u32[]{:S(2)}) %collective-permute-start.1) | collective-permute-done | bytes 270368 | tf_op jit(solution)/shard_map/ppermute | solution.py:287
  28.9 0.0 collective-permute-done.4
  29.0 0.1 collective-permute-start.5
  29.1 0.1 pad_add_fusion.place
  29.2 3.5 %shard_map.111.refs_3_.refs_1_ = bf16[2,2048,768]{2,1,0:T(8,128)(2,1)S(1)} custom-call(s32[4]{0:T(128)S(1)} %pad_add_fusion.place, bf16[8,2048,384]{2,1,0:T(8,128)(2,1)} %refs_0_.4, bf16[8,2048,384]{2,1,0:T(8,128)(2,1)} %refs_1_.3), custom_call_target="tpu_custom_call" | custom-call | flops 3145728 | bytes 12582912 | tf_op jit(solution)/shard_map/pallas_call | solution.py:342
  32.6 3.5 %shard_map.110.refs_2_.refs_0_ = bf16[2,2048,768]{2,1,0:T(8,128)(2,1)S(1)} custom-call(s32[4]{0:T(128)S(1)} %pad_add_fusion.place, bf16[8,2048,384]{2,1,0:T(8,128)(2,1)} %refs_0_.4, bf16[8,2048,384]{2,1,0:T(8,128)(2,1)} %refs_1_.3), custom_call_target="tpu_custom_call" | custom-call | flops 3145728 | bytes 12582912 | tf_op jit(solution)/shard_map/pallas_call | solution.py:342
  36.1 0.0 copy-start
  36.1 3.5 %shard_map.112.refs_4_ = bf16[4,2048,384]{2,1,0:T(8,128)(2,1)S(1)} custom-call(s32[4]{0:T(128)S(1)} %pad_add_fusion.place, bf16[8,2048,384]{2,1,0:T(8,128)(2,1)} %refs_0_.5), custom_call_target="tpu_custom_call" | custom-call | flops 3145728 | bytes 12582912 | tf_op jit(solution)/shard_map/pallas_call | solution.py:342
  39.5 0.0 copy-done
  39.5 0.1 pad_maximum_fusion
  39.7 0.7 pad_maximum_fusion.2
  40.4 1.5 %collective-permute-start.7 = (bf16[4,16,2176]{2,1,0:T(8,128)(2,1)}, bf16[4,16,2176]{2,1,0:T(8,128)(2,1)}, u32[]{:S(2)}, u32[]{:S(2)}) collective-permute-start(bf16[4,16,2176]{2,1,0:T(8,128)(2,1)} %pad_maximum_fusion.2), channel_id=1, source_target_pairs={{0,16},{1,17},{2,18},{3,19},{4,20},{5,21},{6,22},{7,23},{8,24},{9,... | collective-permute-start | bytes 835592 | tf_op jit(solution)/shard_map/ppermute | solution.py:287
  41.9 0.0 collective-permute-done.5.refs_1_
  41.9 5.0 %hidden.1 = (bf16[256,1152]{1,0:T(8,128)(2,1)S(1)}, bf16[256,256]{1,0:T(8,128)(2,1)S(1)}, f32[4,8,256]{2,1,0:T(8,128)S(1)}) custom-call(s32[4]{0:T(128)S(1)} %pad_add_fusion.place, bf16[8,16,4224]{2,1,0:T(8,128)(2,1)S(1)} %constant_dynamic-update-slice_fusion.refs_0_, bf16[8,16,4224]{2,1,0:T(8,128)(2,1)S(1)} %collective-permute-done.5.refs_1_, ...), custom_call_target="tpu_custom_call" | custom-call | flops 1207959552 | bytes 18874368 | tf_op jit(solution)/shard_map/hidden/pallas_call | solution.py:356
  46.9 4.8 %contributions.1 = (bf16[8,16,2176]{2,1,0:T(8,128)(2,1)S(1)}, bf16[8,16,2176]{2,1,0:T(8,128)(2,1)S(1)}) custom-call(s32[4]{0:T(128)S(1)} %pad_add_fusion.place, bf16[256,1152]{1,0:T(8,128)(2,1)S(1)} %get-tuple-element.15.hidden, bf16[256,256]{1,0:T(8,128)(2,1)S(1)} %get-tuple-element.16.chosen, f32[4,8,256]{2,1,0:T(8,128)S(1)} %get-tuple-element.17.prob, ...), custom_call_target="tpu_custom_call" | custom-call | flops 1610612736 | bytes 12582912 | tf_op jit(solution)/shard_map/contributions/pallas_call | solution.py:394
  51.7 0.3 collective-permute-start.6
  52.0 0.1 pad_maximum_fusion.1
  52.1 0.0 copy-start.1
  52.1 0.8 constant_dynamic-slice_fusion.1
  52.9 0.5 collective-permute-start.12
  53.4 0.0 collective-permute-start.11
  53.4 0.3 collective-permute-done.6
  53.7 0.0 copy-done.1
  53.7 0.0 slice-start
  53.7 0.9 %add_convert_fusion = bf16[8,16,2176]{2,1,0:T(8,128)(2,1)} fusion(bf16[8,16,2176]{2,1,0:T(8,128)(2,1)S(1)} %collective-permute-done.6, bf16[8,16,2176]{2,1,0:T(8,128)(2,1)S(1)} %get-tuple-element.18), kind=kLoop, calls=%fused_computation | loop fusion | flops 1114112 | bytes 1671168 | tf_op jit(solution)/shard_map/convert_element_type | solution.py:407
  54.6 4.4 %all-to-all-start = ((bf16[8,16,2176]{2,1,0:T(8,128)(2,1)}), bf16[8,16,2176]{2,1,0:T(8,128)(2,1)}, u32[]{:S(2)}, u32[]{:S(2)}) async-start(bf16[8,16,2176]{2,1,0:T(8,128)(2,1)} %add_convert_fusion), calls=%async_computation | async-start | bytes 1114112 | tf_op jit(solution)/shard_map/all_to_all | solution.py:410
  59.0 9.3 %collective-permute-done.12 = bf16[256,1152]{1,0:T(8,128)(2,1)S(1)} collective-permute-done((bf16[256,1152]{1,0:T(8,128)(2,1)S(1)}, bf16[256,1152]{1,0:T(8,128)(2,1)S(1)}, u32[]{:S(2)}, u32[]{:S(2)}) %collective-permute-start.12) | collective-permute-done | bytes 589856 | tf_op jit(solution)/shard_map/ppermute | solution.py:287
  68.3 0.0 collective-permute-start.13
  68.3 0.0 slice-done
  68.3 0.9 %pad_maximum_fusion.3 = bf16[4,16,2176]{2,1,0:T(8,128)(2,1)S(1)} fusion(bf16[4,16,128]{2,1,0:T(8,128)(2,1)S(1)} %slice-done, bf16[4,16,1024]{2,1,0:T(8,128)(2,1)} %get-tuple-element.26, bf16[4,16,1024]{2,1,0:T(8,128)(2,1)S(1)} %get-tuple-element.25), kind=kLoop, calls=%fused_computation.4 | loop fusion | flops 835584 | bytes 557056 | tf_op jit(solution)/shard_map/concatenate | solution.py:315
  69.3 0.6 collective-permute-start.8
  69.8 0.0 collective-permute-done.7.refs_2_
  69.8 0.2 collective-permute-start.9
  70.1 8.3 %collective-permute-done.8.refs_3_ = bf16[4,16,2176]{2,1,0:T(8,128)(2,1)S(1)} collective-permute-done((bf16[4,16,2176]{2,1,0:T(8,128)(2,1)S(1)}, bf16[4,16,2176]{2,1,0:T(8,128)(2,1)S(1)}, u32[]{:S(2)}, u32[]{:S(2)}) %collective-permute-start.8) | collective-permute-done | bytes 278560 | tf_op jit(solution)/shard_map/ppermute | solution.py:287
  78.4 0.0 collective-permute-start.10
  78.4 0.1 pad_add_fusion.1.place
  78.5 0.0 collective-permute-done.9.refs_4_
  78.5 1.5 %collective-permute-done.10.refs_5_ = bf16[4,16,2176]{2,1,0:T(8,128)(2,1)S(1)} collective-permute-done((bf16[4,16,2176]{2,1,0:T(8,128)(2,1)S(1)}, bf16[4,16,2176]{2,1,0:T(8,128)(2,1)S(1)}, u32[]{:S(2)}, u32[]{:S(2)}) %collective-permute-start.10) | collective-permute-done | bytes 278560 | tf_op jit(solution)/shard_map/ppermute | solution.py:287
  80.0 0.0 collective-permute-done.11
  80.0 0.0 collective-permute-done.13
  80.0 9.5 %weight_grads.1 = (f32[8,512,384]{2,1,0:T(8,128)}, f32[8,512,384]{2,1,0:T(8,128)}, f32[8,512,384]{2,1,0:T(8,128)}) custom-call(s32[4]{0:T(128)S(1)} %pad_add_fusion.1.place, bf16[8,16,4224]{2,1,0:T(8,128)(2,1)S(1)} %constant_dynamic-update-slice_fusion.refs_0_, bf16[8,16,4224]{2,1,0:T(8,128)(2,1)S(1)} %collective-permute-done.5.refs_1_, ...), custom_call_target="tpu_custom_call" | custom-call | flops 1207959552 | bytes 18874368 | tf_op jit(solution)/shard_map/weight_grads/pallas_call | solution.py:414
  89.5 0.0 all-to-all-done.back
  89.5 1.9 %finish.1 = (bf16[16,2048]{1,0:T(8,128)(2,1)}, bf16[8,16]{1,0:T(8,128)(2,1)}) custom-call(s32[8,16]{1,0:T(8,128)} %bitcast.33, bf16[8,16,2176]{2,1,0:T(8,128)(2,1)} %all-to-all-done.back), custom_call_target="tpu_custom_call" | custom-call | tf_op jit(solution)/shard_map/finish/pallas_call | solution.py:443
  (9 shorter events, 0.2 us)
Async XLA Ops:
  2.2 9.8 %collective-permute-start.3 = (bf16[16,4224]{1,0:T(8,128)(2,1)}, bf16[16,4224]{1,0:T(8,128)(2,1)S(1)}, u32[]{:S(2)}, u32[]{:S(2)}) collective-permute-start(bf16[16,4224]{1,0:T(8,128)(2,1)} %pack.1), channel_id=1, source_target_pairs={{0,6},{1,7},{2,4},{3,5},{4,2},{5,3},{6,0},{7,1},{8,14},{9,15},{10,... | collective-permute-start | bytes 405512 | tf_op jit(solution)/shard_map/ppermute | solution.py:287
  7.3 11.6 %collective-permute-start.2 = (bf16[16,4224]{1,0:T(8,128)(2,1)}, bf16[16,4224]{1,0:T(8,128)(2,1)S(1)}, u32[]{:S(2)}, u32[]{:S(2)}) collective-permute-start(bf16[16,4224]{1,0:T(8,128)(2,1)} %pack.1), channel_id=1, source_target_pairs={{0,4},{1,5},{2,6},{3,7},{4,0},{5,1},{6,2},{7,3},{8,12},{9,13},{10,... | collective-permute-start | bytes 405512 | tf_op jit(solution)/shard_map/ppermute | solution.py:287
  7.3 13.3 %collective-permute-start = (bf16[16,4224]{1,0:T(8,128)(2,1)}, bf16[16,4224]{1,0:T(8,128)(2,1)S(1)}, u32[]{:S(2)}, u32[]{:S(2)}) collective-permute-start(bf16[16,4224]{1,0:T(8,128)(2,1)} %pack.1), channel_id=1, source_target_pairs={{0,1},{1,0},{2,3},{3,2},{4,5},{5,4},{6,7},{7,6},{8,9},{9,8},{10,11... | collective-permute-start | bytes 405512 | tf_op jit(solution)/shard_map/ppermute | solution.py:287
  19.0 9.9 %collective-permute-start.4 = (bf16[2,16,4224]{2,1,0:T(8,128)(2,1)S(1)}, bf16[2,16,4224]{2,1,0:T(8,128)(2,1)S(1)}, u32[]{:S(2)}, u32[]{:S(2)}) collective-permute-start(bf16[2,16,4224]{2,1,0:T(8,128)(2,1)S(1)} %pad_maximum_fusion.5), channel_id=1, source_target_pairs={{0,1},{1,0},{2,3},{3,2},{4,5},{5,4},{6,7},{7,6},{8,9},{9,8},{10,11... | collective-permute-start | bytes 811016 | tf_op jit(solution)/shard_map/ppermute | solution.py:287
  21.5 7.3 %collective-permute-start.1 = (bf16[2,16,4224]{2,1,0:T(8,128)(2,1)S(1)}, bf16[2,16,4224]{2,1,0:T(8,128)(2,1)S(1)}, u32[]{:S(2)}, u32[]{:S(2)}) collective-permute-start(bf16[2,16,4224]{2,1,0:T(8,128)(2,1)S(1)} %pad_maximum_fusion.4), channel_id=1, source_target_pairs={{0,2},{1,3},{2,0},{3,1},{4,6},{5,7},{6,4},{7,5},{8,10},{9,11},{10,... | collective-permute-start | bytes 811016 | tf_op jit(solution)/shard_map/ppermute | solution.py:287
  29.0 12.9 %collective-permute-start.5 = (bf16[8,16,4224]{2,1,0:T(8,128)(2,1)S(1)}, bf16[8,16,4224]{2,1,0:T(8,128)(2,1)S(1)}, u32[]{:S(2)}, u32[]{:S(2)}) collective-permute-start(bf16[8,16,4224]{2,1,0:T(8,128)(2,1)S(1)} %constant_dynamic-update-slice_fusion.refs_0_), channel_id=1, source_target_pairs={{0,8},{1,9},{2,10},{3,11},{4,12},{5,13},{6,14},{7,15},{8,0},{9,1},... | collective-permute-start | bytes 3244040 | tf_op jit(solution)/shard_map/ppermute | solution.py:287
  36.1 3.5 %copy-start = (bf16[16,4224]{1,0:T(8,128)(2,1)S(1)}, bf16[16,4224]{1,0:T(8,128)(2,1)}, u32[]{:S(2)}) copy-start(bf16[16,4224]{1,0:T(8,128)(2,1)} %pack.1) | copy-start | bytes 405508
  40.4 29.4 %collective-permute-start.7 = (bf16[4,16,2176]{2,1,0:T(8,128)(2,1)}, bf16[4,16,2176]{2,1,0:T(8,128)(2,1)}, u32[]{:S(2)}, u32[]{:S(2)}) collective-permute-start(bf16[4,16,2176]{2,1,0:T(8,128)(2,1)} %pad_maximum_fusion.2), channel_id=1, source_target_pairs={{0,16},{1,17},{2,18},{3,19},{4,20},{5,21},{6,22},{7,23},{8,24},{9,... | collective-permute-start | bytes 835592 | tf_op jit(solution)/shard_map/ppermute | solution.py:287
  51.7 2.0 %collective-permute-start.6 = (bf16[8,16,2176]{2,1,0:T(8,128)(2,1)S(1)}, bf16[8,16,2176]{2,1,0:T(8,128)(2,1)S(1)}, u32[]{:S(2)}, u32[]{:S(2)}) collective-permute-start(bf16[8,16,2176]{2,1,0:T(8,128)(2,1)S(1)} %get-tuple-element.19), channel_id=1, source_target_pairs={{0,8},{1,9},{2,10},{3,11},{4,12},{5,13},{6,14},{7,15},{8,0},{9,1},... | collective-permute-start | bytes 1671176 | tf_op jit(solution)/shard_map/ppermute | solution.py:287
  52.1 1.6 %copy-start.1 = (bf16[4,16,4224]{2,1,0:T(8,128)(2,1)}, bf16[4,16,4224]{2,1,0:T(8,128)(2,1)S(1)}, u32[]{:S(2)}) copy-start(bf16[4,16,4224]{2,1,0:T(8,128)(2,1)S(1)} %pad_maximum_fusion.1) | copy-start | bytes 1622020
  52.9 15.5 %collective-permute-start.12 = (bf16[256,1152]{1,0:T(8,128)(2,1)S(1)}, bf16[256,1152]{1,0:T(8,128)(2,1)S(1)}, u32[]{:S(2)}, u32[]{:S(2)}) collective-permute-start(bf16[256,1152]{1,0:T(8,128)(2,1)S(1)} %get-tuple-element.15.hidden), channel_id=1, source_target_pairs={{0,16},{1,17},{2,18},{3,19},{4,20},{5,21},{6,22},{7,23},{8,24},{9,... | collective-permute-start | bytes 1769480 | tf_op jit(solution)/shard_map/ppermute | solution.py:287
  53.4 26.6 %collective-permute-start.11 = (bf16[256,1152]{1,0:T(8,128)(2,1)S(1)}, bf16[256,1152]{1,0:T(8,128)(2,1)}, u32[]{:S(2)}, u32[]{:S(2)}) collective-permute-start(bf16[256,1152]{1,0:T(8,128)(2,1)S(1)} %get-tuple-element.15.hidden), channel_id=1, source_target_pairs={{0,8},{1,9},{2,10},{3,11},{4,12},{5,13},{6,14},{7,15},{8,0},{9,1},... | collective-permute-start | bytes 1769480 | tf_op jit(solution)/shard_map/ppermute | solution.py:287
  53.7 14.7 %slice-start = ((bf16[4,16,4224]{2,1,0:T(8,128)(2,1)}), bf16[4,16,128]{2,1,0:T(8,128)(2,1)S(1)}, s32[]{:S(2)}) async-start(bf16[4,16,4224]{2,1,0:T(8,128)(2,1)} %copy-done.1), calls=%async_computation.1 | async-start | bytes 32768 | tf_op jit(solution)/shard_map/slice | solution.py:319
  54.6 34.9 %all-to-all-start = ((bf16[8,16,2176]{2,1,0:T(8,128)(2,1)}), bf16[8,16,2176]{2,1,0:T(8,128)(2,1)}, u32[]{:S(2)}, u32[]{:S(2)}) async-start(bf16[8,16,2176]{2,1,0:T(8,128)(2,1)} %add_convert_fusion), calls=%async_computation | async-start | bytes 1114112 | tf_op jit(solution)/shard_map/all_to_all | solution.py:410
  68.3 11.6 %collective-permute-start.13 = (bf16[256,1152]{1,0:T(8,128)(2,1)S(1)}, bf16[256,1152]{1,0:T(8,128)(2,1)S(1)}, u32[]{:S(2)}, u32[]{:S(2)}) collective-permute-start(bf16[256,1152]{1,0:T(8,128)(2,1)S(1)} %collective-permute-done.12), channel_id=1, source_target_pairs={{0,8},{1,9},{2,10},{3,11},{4,12},{5,13},{6,14},{7,15},{8,0},{9,1},... | collective-permute-start | bytes 1769480 | tf_op jit(solution)/shard_map/ppermute | solution.py:287
  69.3 9.1 %collective-permute-start.8 = (bf16[4,16,2176]{2,1,0:T(8,128)(2,1)S(1)}, bf16[4,16,2176]{2,1,0:T(8,128)(2,1)S(1)}, u32[]{:S(2)}, u32[]{:S(2)}) collective-permute-start(bf16[4,16,2176]{2,1,0:T(8,128)(2,1)S(1)} %pad_maximum_fusion.3), channel_id=1, source_target_pairs={{0,16},{1,17},{2,18},{3,19},{4,20},{5,21},{6,22},{7,23},{8,24},{9,... | collective-permute-start | bytes 835592 | tf_op jit(solution)/shard_map/ppermute | solution.py:287
  69.8 8.6 %collective-permute-start.9 = (bf16[4,16,2176]{2,1,0:T(8,128)(2,1)}, bf16[4,16,2176]{2,1,0:T(8,128)(2,1)S(1)}, u32[]{:S(2)}, u32[]{:S(2)}) collective-permute-start(bf16[4,16,2176]{2,1,0:T(8,128)(2,1)} %collective-permute-done.7.refs_2_), channel_id=1, source_target_pairs={{0,8},{1,9},{2,10},{3,11},{4,12},{5,13},{6,14},{7,15},{8,0},{9,1},... | collective-permute-start | bytes 835592 | tf_op jit(solution)/shard_map/ppermute | solution.py:287
  78.4 1.6 %collective-permute-start.10 = (bf16[4,16,2176]{2,1,0:T(8,128)(2,1)S(1)}, bf16[4,16,2176]{2,1,0:T(8,128)(2,1)S(1)}, u32[]{:S(2)}, u32[]{:S(2)}) collective-permute-start(bf16[4,16,2176]{2,1,0:T(8,128)(2,1)S(1)} %collective-permute-done.8.refs_3_), channel_id=1, source_target_pairs={{0,8},{1,9},{2,10},{3,11},{4,12},{5,13},{6,14},{7,15},{8,0},{9,1},... | collective-permute-start | bytes 835592 | tf_op jit(solution)/shard_map/ppermute | solution.py:287
